TPU v7x, 32 devices: a whole 2x2x4 slice. The times are simulated.
32 devices in a mesh: groups: 2 (over y), cache: 4 (over x, core), tensor: 4 (over z).
Axes of the slice: x: 2, y: 2, z: 4, core: 2. Of those that a mesh axis runs over, the one named last changes fastest.
Arguments:
- queries: bfloat16 [2048, 8192], P(('groups', 'cache'), 'tensor'), parts along dimension 0, may hold values from -8 to 8
- suffix_key_value: bfloat16 [2, 2048, 1024], P(None, ('groups', 'cache'), 'tensor'), parts along dimension 1, may hold values from -6 to 6
- kv_pages: bfloat16 [768, 2, 128, 1024], P(('groups', 'cache'), None, None, 'tensor'), parts along dimension 0, may hold values from -6 to 6
- page_ids: int32 [8, 64], P(('groups', 'cache')), parts along dimension 0, may hold values from 0 to 383, as said below
- prefix_pages: int32 [8], P(('groups', 'cache')), parts along dimension 0, may hold values from 8 to 64, as said below
- page_home: int32 [768], P('groups'), parts along dimension 0, may hold values from 0 to 383, as said below
- out_weight: bfloat16 [8192, 8192], P('tensor', 'cache'), may hold values from -0.25 to 0.25
Outputs:
- attended: bfloat16 [2048, 8192], P(('groups', 'cache'), 'tensor'), parts along dimension 0
There are 2 independent parts, one for each index of `groups`. A program takes and returns all parts, laid end to end along the dimension named above; an argument that names none is the same for every part. Nothing has to cross between parts.
Inputs may be any that keep to these rules, and one draw needn't show every extreme that they name: `page_ids`: live slots are j < prefix_pages[r]. Within the aligned block of 1 request of one index of cache, no page id appears twice among all 64 slots, and at most 24 of these slots name pages whose row page_home[id] lies on one index of cache (row // 96); in every such block some index of cache gets exactly 24. `prefix_pages`: one request in each draw has 64 pages and another has 8. `page_home`: A permutation of 0 to 383.
All inputs are finite; a program needn't handle non-finite values.
Results may differ from a plain program's by a relative error of at most 0.015.
Values may be sent and summed in bfloat16 or wider, within the bound.
No kernel may reach another device: no remote copies, remote signals or barrier semaphores. Data moves between devices by JAX's collectives and lax.ppermute only.
A program may use at most 128 MiB of HBM per device.

v0:
```python
import jax
import jax.numpy as jnp
from jax import lax
from jax.sharding import PartitionSpec as P

QUERY_HEADS = 64
KEY_VALUE_HEADS = 8
HEAD_SIZE = 128
PAGE_TOKENS = 128
SUF = 256
MAXP = 64


masked_score = -1e30
pages_per_block = 4


def per_device(queries, suffix_key_value, kv_pages, page_ids, prefix_pages, page_home, out_weight):
    cache_count = lax.axis_size("cache")
    request_count = page_ids.shape[0]
    capacity = (3 * request_count * MAXP + 2 * cache_count - 1) // (2 * cache_count)
    pool_rows = kv_pages.shape[0]
    kv_width = kv_pages.shape[3]
    kv_heads_here = kv_width // HEAD_SIZE
    group_width = QUERY_HEADS // KEY_VALUE_HEADS
    score_scale = HEAD_SIZE ** (-0.5)
    table_index = jnp.arange(page_home.shape[0], dtype=jnp.int32)
    owner_index = jnp.arange(cache_count, dtype=jnp.int32)
    buffer_index = jnp.arange(cache_count * capacity, dtype=jnp.int32)
    flat_ids = page_ids.reshape(-1)
    rows_of = jnp.sum(
        jnp.where(flat_ids[:, None] == table_index[None, :], page_home[None, :], 0), axis=1
    )
    owners = rows_of // pool_rows
    within = rows_of % pool_rows
    live_slots = (jnp.arange(MAXP, dtype=jnp.int32)[None, :] < prefix_pages[:, None]).reshape(-1)
    member = ((owners[:, None] == owner_index[None, :]) & live_slots[:, None]).astype(jnp.int32)
    earlier = jnp.cumsum(member, axis=0) - member
    rank_within = jnp.sum(earlier * member, axis=1)
    target = jnp.where(live_slots, owners * capacity + rank_within, -1)
    wanted = jnp.sum(
        jnp.where(target[:, None] == buffer_index[None, :], within[:, None], 0), axis=0
    )
    target, wanted = (target, wanted.reshape(cache_count, capacity))
    slot_ids = lax.all_to_all(wanted, "cache", split_axis=0, concat_axis=0, tiled=True)
    chosen = jnp.take(kv_pages, slot_ids.reshape(-1), axis=0)
    arrived = lax.all_to_all(
        chosen.reshape(slot_ids.shape + kv_pages.shape[1:]),
        "cache",
        split_axis=0,
        concat_axis=0,
        tiled=True,
    )
    buffer = arrived.reshape(cache_count * capacity, 2, PAGE_TOKENS, kv_width)
    fetched = jnp.take(buffer, jnp.maximum(target, 0), axis=0).reshape(
        request_count, MAXP, 2, PAGE_TOKENS, kv_width
    )
    positions = jnp.arange(SUF, dtype=jnp.int32)
    causal = (positions[None, :] <= positions[:, None])[None, :, None, :]
    block_keys = pages_per_block * PAGE_TOKENS
    key_pages = jnp.arange(block_keys, dtype=jnp.int32) // PAGE_TOKENS
    query_block = queries.reshape(SUF, kv_heads_here, group_width, HEAD_SIZE)
    suffix_keys = suffix_key_value[0, 0:SUF].reshape(SUF, kv_heads_here, HEAD_SIZE)
    suffix_values = suffix_key_value[1, 0:SUF].reshape(SUF, kv_heads_here, HEAD_SIZE)
    scores = (
        jnp.einsum("skgd,tkd->ksgt", query_block, suffix_keys, preferred_element_type=jnp.float32)
        * score_scale
    )
    scores = jnp.where(causal, scores, masked_score)
    row_top = jnp.max(scores, axis=3)
    weights = jnp.where(causal, jnp.exp(scores - row_top[..., None]), 0.0)
    weight_sum = jnp.sum(weights, axis=3)
    accumulated = jnp.einsum(
        "ksgt,tkd->ksgd",
        weights.astype(jnp.bfloat16),
        suffix_values,
        preferred_element_type=jnp.float32,
    )
    pages_here = fetched[0]
    length = prefix_pages[0]
    block_count = (length + pages_per_block - 1) // pages_per_block

    def attend_block(block_index, state_now):
        top_now, sum_now, acc_now = state_now
        page_piece = lax.dynamic_slice_in_dim(
            pages_here, block_index * pages_per_block, pages_per_block, 0
        )
        key_rows = page_piece[:, 0].reshape(block_keys, kv_heads_here, HEAD_SIZE)
        value_rows = page_piece[:, 1].reshape(block_keys, kv_heads_here, HEAD_SIZE)
        live_keys = (block_index * pages_per_block + key_pages < length)[None, None, None, :]
        block_scores = (
            jnp.einsum("skgd,tkd->ksgt", query_block, key_rows, preferred_element_type=jnp.float32)
            * score_scale
        )
        block_scores = jnp.where(live_keys, block_scores, masked_score)
        new_top = jnp.maximum(top_now, jnp.max(block_scores, axis=3))
        factor = jnp.exp(top_now - new_top)
        block_weights = jnp.where(live_keys, jnp.exp(block_scores - new_top[..., None]), 0.0)
        new_sum = sum_now * factor + jnp.sum(block_weights, axis=3)
        new_acc = acc_now * factor[..., None] + jnp.einsum(
            "ksgt,tkd->ksgd",
            block_weights.astype(jnp.bfloat16),
            value_rows,
            preferred_element_type=jnp.float32,
        )
        return (new_top, new_sum, new_acc)

    row_top, weight_sum, accumulated = lax.fori_loop(
        0, block_count, attend_block, (row_top, weight_sum, accumulated)
    )
    mixed_heads = (accumulated / weight_sum[..., None]).astype(jnp.bfloat16)
    outputs = jnp.transpose(mixed_heads, (1, 0, 2, 3)).reshape(
        SUF, kv_heads_here * group_width * HEAD_SIZE
    )
    column_terms = jnp.dot(
        lax.all_gather(outputs, "cache", axis=0, tiled=True),
        out_weight,
        preferred_element_type=jnp.float32,
    ).astype(jnp.bfloat16)
    group_term = lax.all_to_all(
        column_terms, "cache", split_axis=0, concat_axis=1, tiled=True
    ).astype(jnp.float32)
    attended = lax.psum_scatter(
        group_term.astype(jnp.bfloat16), "tensor", scatter_dimension=1, tiled=True
    )
    return attended


def solution(mesh):
    in_specs = (
        P(("groups", "cache"), "tensor"),
        P(None, ("groups", "cache"), "tensor"),
        P(("groups", "cache"), None, None, "tensor"),
        P(("groups", "cache"), None),
        P(("groups", "cache")),
        P("groups"),
        P("tensor", "cache"),
    )
    out_specs = P(("groups", "cache"), "tensor")
    return jax.shard_map(
        per_device, mesh=mesh, in_specs=in_specs, out_specs=out_specs, check_vma=False
    )
```

profile of v0, /device:TPU:0, one launch (start us, length us, event | category | flops | bytes accessed | tf_op | source)
XLA Modules:
  0.0 627.7 jit_solution(12260679545356079617)
XLA Ops:
  8.7 7.8 %all_to_all.33 = s32[4,1,24]{2,1,0:T(1,128)S(1)} all-to-all(s32[4,1,24]{2,1,0:T(1,128)S(1)} %bitcast.108), channel_id=1, replica_groups=mesh['groups'=2,'cache'=4,'tensor'=4] {'cache'}, dimensions={0} | all-to-all | bytes 768 | tf_op jit(solution)/shard_map/all_to_all | solution.py:45
  17.8 11.4 %gather_fusion = bf16[96,2,128,256]{3,2,1,0:T(8,128)(2,1)} fusion(bf16[96,2,128,256]{3,2,1,0:T(8,128)(2,1)} %param.11, s32[1024]{0:T(1024)S(1)} %pad_clamp_fusion.1), kind=kCustom, calls=%fused_computation | custom fusion | bytes 25166208 | tf_op jit(solution)/shard_map/jit(_take)/gather | solution.py:46
  29.1 10.9 %broadcast_select_fusion = bf16[4,24,2,128,256]{4,3,2,1,0:T(8,128)(2,1)} fusion(bf16[4,24,2,128,256]{4,3,2,1,0:T(8,128)(2,1)} %bitcast.96, pred[4,24]{1,0:T(4,128)(4,1)S(1)} %compare_and_fusion), kind=kLoop, calls=%fused_computation.33 | loop fusion | flops 6291456 | bytes 25165920 | tf_op jit(solution)/shard_map/jit(_take)/select_n | solution.py:46
  52.8 131.8 %all-to-all-done.1 = bf16[4,24,2,128,256]{4,3,2,1,0:T(8,128)(2,1)} async-done(((bf16[4,24,2,128,256]{4,3,2,1,0:T(8,128)(2,1)}), bf16[4,24,2,128,256]{4,3,2,1,0:T(8,128)(2,1)}, u32[]{:S(2)}, u32[]{:S(2)}) %all-to-all-start.1) | async-done | bytes 12582944 | tf_op jit(solution)/shard_map/all_to_all | solution.py:47
  184.5 10.1 %gather_fusion.1 = bf16[64,2,128,256]{3,2,1,0:T(8,128)(2,1)} fusion(bf16[96,2,128,256]{3,2,1,0:T(8,128)(2,1)} %bitcast.11, s32[1024]{0:T(1024)S(1)} %pad_clamp_fusion), kind=kCustom, calls=%fused_computation.1 | custom fusion | bytes 16777472 | tf_op jit(solution)/shard_map/jit(_take)/gather | solution.py:55
  194.6 7.4 %broadcast_select_fusion.1 = bf16[64,2,128,256]{3,2,1,0:T(8,128)(2,1)} fusion(bf16[64,2,128,256]{3,2,1,0:T(8,128)(2,1)} %gather_fusion.1, pred[64]{0:T(512)(128)(4,1)S(1)} %get-tuple-element.125), kind=kLoop, calls=%fused_computation.34 | loop fusion | flops 4194304 | bytes 16777280 | tf_op jit(solution)/shard_map/jit(_take)/select_n | solution.py:55
  202.1 193.0 %while.15 = (s32[]{:T(128)}, f32[2,256,8]{1,2,0:T(8,128)S(1)}, f32[2,256,8]{1,2,0:T(8,128)S(1)}, f32[2,256,8,128]{3,1,2,0:T(8,128)}, s32[]{:T(128)}, /*index=5*/...) while((s32[]{:T(128)}, f32[2,256,8]{1,2,0:T(8,128)S(1)}, ...), condition=%wide.region_9.10_spmd.clone, body=%wide.region_6.9_spmd.clone.sunk | while | flops 1102066688 | bytes 66848992 | solution.py:108
  208.5 8.4 %multiply_add_fusion.5 = f32[2,256,8,128]{3,1,2,0:T(8,128)} fusion(f32[2,256,8,128]{3,1,2,0:T(8,128)} %get-tuple-element.216, f32[2,512,256,8]{2,1,3,0:T(8,128)} %copy-done, f32[2,256,8]{1,2,0:T(8,128)S(1)} %max.26, pred[512]{0:T(512)(128)(4,1)S(1)} %fusion.58, f32[2,256,8]{1,2,0:T(8,128)S(1)} %get-tuple-element.198, ...), kind=kOutput, calls=%fused_computation.13.clone.1 | convolution fusion | flops 548405248 | bytes 12878336 | tf_op jit(solution)/shard_map/while/body/ksgt,tkd->ksgd/dot_general | solution.py:100
  223.4 8.4 %multiply_add_fusion.5 = f32[2,256,8,128]{3,1,2,0:T(8,128)} fusion(f32[2,256,8,128]{3,1,2,0:T(8,128)} %get-tuple-element.216, f32[2,512,256,8]{2,1,3,0:T(8,128)} %copy-done, f32[2,256,8]{1,2,0:T(8,128)S(1)} %max.26, pred[512]{0:T(512)(128)(4,1)S(1)} %fusion.58, f32[2,256,8]{1,2,0:T(8,128)S(1)} %get-tuple-element.198, ...), kind=kOutput, calls=%fused_computation.13.clone.1 | convolution fusion | flops 548405248 | bytes 12878336 | tf_op jit(solution)/shard_map/while/body/ksgt,tkd->ksgd/dot_general | solution.py:100
  238.2 8.4 %multiply_add_fusion.5 = f32[2,256,8,128]{3,1,2,0:T(8,128)} fusion(f32[2,256,8,128]{3,1,2,0:T(8,128)} %get-tuple-element.216, f32[2,512,256,8]{2,1,3,0:T(8,128)} %copy-done, f32[2,256,8]{1,2,0:T(8,128)S(1)} %max.26, pred[512]{0:T(512)(128)(4,1)S(1)} %fusion.58, f32[2,256,8]{1,2,0:T(8,128)S(1)} %get-tuple-element.198, ...), kind=kOutput, calls=%fused_computation.13.clone.1 | convolution fusion | flops 548405248 | bytes 12878336 | tf_op jit(solution)/shard_map/while/body/ksgt,tkd->ksgd/dot_general | solution.py:100
  253.1 8.4 %multiply_add_fusion.5 = f32[2,256,8,128]{3,1,2,0:T(8,128)} fusion(f32[2,256,8,128]{3,1,2,0:T(8,128)} %get-tuple-element.216, f32[2,512,256,8]{2,1,3,0:T(8,128)} %copy-done, f32[2,256,8]{1,2,0:T(8,128)S(1)} %max.26, pred[512]{0:T(512)(128)(4,1)S(1)} %fusion.58, f32[2,256,8]{1,2,0:T(8,128)S(1)} %get-tuple-element.198, ...), kind=kOutput, calls=%fused_computation.13.clone.1 | convolution fusion | flops 548405248 | bytes 12878336 | tf_op jit(solution)/shard_map/while/body/ksgt,tkd->ksgd/dot_general | solution.py:100
  267.9 8.4 %multiply_add_fusion.5 = f32[2,256,8,128]{3,1,2,0:T(8,128)} fusion(f32[2,256,8,128]{3,1,2,0:T(8,128)} %get-tuple-element.216, f32[2,512,256,8]{2,1,3,0:T(8,128)} %copy-done, f32[2,256,8]{1,2,0:T(8,128)S(1)} %max.26, pred[512]{0:T(512)(128)(4,1)S(1)} %fusion.58, f32[2,256,8]{1,2,0:T(8,128)S(1)} %get-tuple-element.198, ...), kind=kOutput, calls=%fused_computation.13.clone.1 | convolution fusion | flops 548405248 | bytes 12878336 | tf_op jit(solution)/shard_map/while/body/ksgt,tkd->ksgd/dot_general | solution.py:100
  282.7 8.4 %multiply_add_fusion.5 = f32[2,256,8,128]{3,1,2,0:T(8,128)} fusion(f32[2,256,8,128]{3,1,2,0:T(8,128)} %get-tuple-element.216, f32[2,512,256,8]{2,1,3,0:T(8,128)} %copy-done, f32[2,256,8]{1,2,0:T(8,128)S(1)} %max.26, pred[512]{0:T(512)(128)(4,1)S(1)} %fusion.58, f32[2,256,8]{1,2,0:T(8,128)S(1)} %get-tuple-element.198, ...), kind=kOutput, calls=%fused_computation.13.clone.1 | convolution fusion | flops 548405248 | bytes 12878336 | tf_op jit(solution)/shard_map/while/body/ksgt,tkd->ksgd/dot_general | solution.py:100
  297.6 8.4 %multiply_add_fusion.5 = f32[2,256,8,128]{3,1,2,0:T(8,128)} fusion(f32[2,256,8,128]{3,1,2,0:T(8,128)} %get-tuple-element.216, f32[2,512,256,8]{2,1,3,0:T(8,128)} %copy-done, f32[2,256,8]{1,2,0:T(8,128)S(1)} %max.26, pred[512]{0:T(512)(128)(4,1)S(1)} %fusion.58, f32[2,256,8]{1,2,0:T(8,128)S(1)} %get-tuple-element.198, ...), kind=kOutput, calls=%fused_computation.13.clone.1 | convolution fusion | flops 548405248 | bytes 12878336 | tf_op jit(solution)/shard_map/while/body/ksgt,tkd->ksgd/dot_general | solution.py:100
  312.4 8.4 %multiply_add_fusion.5 = f32[2,256,8,128]{3,1,2,0:T(8,128)} fusion(f32[2,256,8,128]{3,1,2,0:T(8,128)} %get-tuple-element.216, f32[2,512,256,8]{2,1,3,0:T(8,128)} %copy-done, f32[2,256,8]{1,2,0:T(8,128)S(1)} %max.26, pred[512]{0:T(512)(128)(4,1)S(1)} %fusion.58, f32[2,256,8]{1,2,0:T(8,128)S(1)} %get-tuple-element.198, ...), kind=kOutput, calls=%fused_computation.13.clone.1 | convolution fusion | flops 548405248 | bytes 12878336 | tf_op jit(solution)/shard_map/while/body/ksgt,tkd->ksgd/dot_general | solution.py:100
  327.3 8.4 %multiply_add_fusion.5 = f32[2,256,8,128]{3,1,2,0:T(8,128)} fusion(f32[2,256,8,128]{3,1,2,0:T(8,128)} %get-tuple-element.216, f32[2,512,256,8]{2,1,3,0:T(8,128)} %copy-done, f32[2,256,8]{1,2,0:T(8,128)S(1)} %max.26, pred[512]{0:T(512)(128)(4,1)S(1)} %fusion.58, f32[2,256,8]{1,2,0:T(8,128)S(1)} %get-tuple-element.198, ...), kind=kOutput, calls=%fused_computation.13.clone.1 | convolution fusion | flops 548405248 | bytes 12878336 | tf_op jit(solution)/shard_map/while/body/ksgt,tkd->ksgd/dot_general | solution.py:100
  342.1 8.4 %multiply_add_fusion.5 = f32[2,256,8,128]{3,1,2,0:T(8,128)} fusion(f32[2,256,8,128]{3,1,2,0:T(8,128)} %get-tuple-element.216, f32[2,512,256,8]{2,1,3,0:T(8,128)} %copy-done, f32[2,256,8]{1,2,0:T(8,128)S(1)} %max.26, pred[512]{0:T(512)(128)(4,1)S(1)} %fusion.58, f32[2,256,8]{1,2,0:T(8,128)S(1)} %get-tuple-element.198, ...), kind=kOutput, calls=%fused_computation.13.clone.1 | convolution fusion | flops 548405248 | bytes 12878336 | tf_op jit(solution)/shard_map/while/body/ksgt,tkd->ksgd/dot_general | solution.py:100
  357.0 8.4 %multiply_add_fusion.5 = f32[2,256,8,128]{3,1,2,0:T(8,128)} fusion(f32[2,256,8,128]{3,1,2,0:T(8,128)} %get-tuple-element.216, f32[2,512,256,8]{2,1,3,0:T(8,128)} %copy-done, f32[2,256,8]{1,2,0:T(8,128)S(1)} %max.26, pred[512]{0:T(512)(128)(4,1)S(1)} %fusion.58, f32[2,256,8]{1,2,0:T(8,128)S(1)} %get-tuple-element.198, ...), kind=kOutput, calls=%fused_computation.13.clone.1 | convolution fusion | flops 548405248 | bytes 12878336 | tf_op jit(solution)/shard_map/while/body/ksgt,tkd->ksgd/dot_general | solution.py:100
  371.8 8.4 %multiply_add_fusion.5 = f32[2,256,8,128]{3,1,2,0:T(8,128)} fusion(f32[2,256,8,128]{3,1,2,0:T(8,128)} %get-tuple-element.216, f32[2,512,256,8]{2,1,3,0:T(8,128)} %copy-done, f32[2,256,8]{1,2,0:T(8,128)S(1)} %max.26, pred[512]{0:T(512)(128)(4,1)S(1)} %fusion.58, f32[2,256,8]{1,2,0:T(8,128)S(1)} %get-tuple-element.198, ...), kind=kOutput, calls=%fused_computation.13.clone.1 | convolution fusion | flops 548405248 | bytes 12878336 | tf_op jit(solution)/shard_map/while/body/ksgt,tkd->ksgd/dot_general | solution.py:100
  386.7 8.4 %multiply_add_fusion.5 = f32[2,256,8,128]{3,1,2,0:T(8,128)} fusion(f32[2,256,8,128]{3,1,2,0:T(8,128)} %get-tuple-element.216, f32[2,512,256,8]{2,1,3,0:T(8,128)} %copy-done, f32[2,256,8]{1,2,0:T(8,128)S(1)} %max.26, pred[512]{0:T(512)(128)(4,1)S(1)} %fusion.58, f32[2,256,8]{1,2,0:T(8,128)S(1)} %get-tuple-element.198, ...), kind=kOutput, calls=%fused_computation.13.clone.1 | convolution fusion | flops 548405248 | bytes 12878336 | tf_op jit(solution)/shard_map/while/body/ksgt,tkd->ksgd/dot_general | solution.py:100
  398.2 80.1 %all-gather.2.cloned.1.call-done = bf16[1024,2048]{0,1:T(8,128)(2,1)} async-done(((bf16[256,2048]{0,1:T(8,128)(2,1)}), bf16[1024,2048]{0,1:T(8,128)(2,1)}) %all-gather.2.cloned.1.call-update) | async-done | bytes 4194320 | tf_op jit(solution)/shard_map/all_gather | solution.py:116
  478.3 12.7 %convolution_convert_fusion = bf16[1024,2048]{1,0:T(8,128)(2,1)S(1)} fusion(bf16[1024,2048]{0,1:T(8,128)(2,1)} %all-gather.2.cloned.1.call-done, bf16[2048,2048]{1,0:T(8,128)(2,1)} %param.15), kind=kOutput, calls=%fused_computation.37 | convolution fusion | flops 8592031744 | bytes 16777216 | tf_op jit(solution)/shard_map/dot_general | solution.py:115
  491.0 50.7 %all_to_all.34 = bf16[4,256,2048]{2,1,0:T(8,128)(2,1)S(1)} all-to-all(bf16[4,256,2048]{2,1,0:T(8,128)(2,1)S(1)} %bitcast.104), channel_id=1, replica_groups=mesh['groups'=2,'cache'=4,'tensor'=4] {'cache'}, dimensions={0} | all-to-all | bytes 8388608 | tf_op jit(solution)/shard_map/all_to_all | solution.py:120
  543.9 77.0 %reduce-scatter.2.cloned.1.call-done = bf16[256,2048]{1,0:T(8,128)(2,1)} async-done(((bf16[256,8192]{1,0:T(8,128)(2,1)}), bf16[256,2048]{1,0:T(8,128)(2,1)}) %reduce-scatter.2.cloned.1.call-update) | async-done | bytes 1048592 | tf_op jit(solution)/shard_map/reduce_scatter | solution.py:123
  (181 shorter events, 104.0 us)
Async XLA Ops:
  40.0 6.5 %copy-start.1 = (bf16[256,2048]{1,0:T(8,128)(2,1)S(1)}, bf16[256,2048]{1,0:T(8,128)(2,1)}, u32[]{:S(2)}) copy-start(bf16[256,2048]{1,0:T(8,128)(2,1)} %param.9) | copy-start | bytes 3145732
  40.0 7.1 %copy-start.2 = (bf16[2,256,256]{2,1,0:T(8,128)(2,1)S(1)}, bf16[2,256,256]{2,1,0:T(8,128)(2,1)}, u32[]{:S(2)}) copy-start(bf16[2,256,256]{2,1,0:T(8,128)(2,1)} %param.10) | copy-start | bytes 786436
  40.0 144.6 %all-to-all-start.1 = ((bf16[4,24,2,128,256]{4,3,2,1,0:T(8,128)(2,1)}), bf16[4,24,2,128,256]{4,3,2,1,0:T(8,128)(2,1)}, u32[]{:S(2)}, u32[]{:S(2)}) async-start(bf16[4,24,2,128,256]{4,3,2,1,0:T(8,128)(2,1)} %broadcast_select_fusion), calls=%async_computation.1 | async-start | bytes 25165824 | tf_op jit(solution)/shard_map/all_to_all | solution.py:47
  46.5 431.8 %all-gather.2.cloned.1.call-start = ((), (), s32[]{:S(2)}) async-start(), calls=%async_computation.4 | async-start | bytes 5242880 | tf_op jit(solution)/shard_map/all_gather | solution.py:116
  205.2 3.2 copy-start
  220.1 3.2 copy-start
  234.9 3.2 copy-start
  249.8 3.2 copy-start
  264.6 3.2 copy-start
  279.4 3.2 copy-start
  294.3 3.2 copy-start
  309.1 3.2 copy-start
  324.0 3.2 copy-start
  338.8 3.2 copy-start
  353.7 3.2 copy-start
  368.5 3.2 copy-start
  383.4 3.2 copy-start
  398.2 222.7 %reduce-scatter.2.cloned.1.call-start = ((), (), s32[]{:S(2)}) async-start(), calls=%async_computation.5 | async-start | bytes 5242880 | tf_op jit(solution)/shard_map/reduce_scatter | solution.py:123
Sparse Core Ops, SparseCore 0:
  398.3 79.9 all-gather.1
  544.1 76.7 reduce-scatter.1
where the time goes:
time: 629 us; the launch traced here: 628 us
  waiting for transfers between devices  289 us (46%)
  matrix products  143 us (23%)
  other arithmetic  61.5 us (10%)
  blocking collectives  58.5 us (9%)
  local copies, waits for them, and re-layouts  54.6 us (9%)
  between operations  14.3 us (2%)
  starting transfers between devices  6.55 us (1%)
    all_to_all x1, waiting for transfers between devices, per_device(): lax.all_to_all(chosen.reshape(slot_ids.shape + kv_pages.shape[1:]), 'cach...  132 us
    dot_general x13, matrix products, attend_block(): jnp.einsum('ksgt,tkd->ksgd', block_weights.astype(jnp.bfloat16), value_ro...  109 us
    all_gather x1, waiting for transfers between devices, per_device(): lax.all_gather(outputs, 'cache', axis=0, tiled=True)  80.1 us
    reduce_scatter x1, waiting for transfers between devices, per_device(): lax.psum_scatter(group_term.astype(jnp.bfloat16), 'tensor', scatter_dimen...  77 us
    all_to_all x1, blocking collectives, per_device(): lax.all_to_all(column_terms, 'cache', split_axis=0, concat_axis=1, tiled=...  50.7 us
    reduce_sum x13, other arithmetic, attend_block(): new_sum = sum_now * factor + jnp.sum(block_weights, axis=3)  30.2 us
    while x52, local copies, waits for them, and re-layouts  25.2 us
    dot_general x13, matrix products, attend_block(): jnp.einsum('skgd,tkd->ksgt', query_block, key_rows, preferred_element_typ...  17.4 us
  transfers between devices with their start and end apart: 3, of which 3 were waited for; matrix products, arithmetic and copies ran while one was open for 1% of the time, Pallas kernels for 0%

commit v1 on v0

v1 whole, which is shorter than its diff:
```python
import functools

import jax
import jax.numpy as jnp
from jax import lax
from jax.experimental import pallas as pl
from jax.experimental.pallas import tpu as pltpu
from jax.sharding import PartitionSpec as P


HEAD_SIZE = 128

nothing = -1e30
pages_per_block = 4
token_pieces = 2
log2_e = 1.4426950408889634


def attend_kernel(which, lists, counts, token, *refs, parts, kv_heads, heads, tokens, first_token, suffix):
    queries, refs = refs[:parts], refs[parts:]
    pages, refs = refs[0], refs[1:]
    if suffix:
        suffix_kv, refs = refs[0], refs[1:]
    outs, lses, refs = refs[:parts], refs[parts : 2 * parts], refs[2 * parts :]
    q, q_sems, buf, sems, top_s, sum_s, acc_s = refs
    page_tokens = pages.shape[2]
    rows = heads * tokens
    factor = HEAD_SIZE ** (-0.5) * log2_e
    block_keys = pages_per_block * page_tokens

    def live_of(part):
        return counts[which[part]]

    def blocks_of(part):
        return (live_of(part) + pages_per_block - 1) // pages_per_block

    def copy_of(part, block, slot, place):
        row = lists[which[part], block * pages_per_block + place]
        return pltpu.make_async_copy(pages.at[row], buf.at[slot, place], sems.at[slot, place])

    def start(part, block, slot):
        for place in range(pages_per_block):
            copy_of(part, block, slot, place).start()

    def query_copy(part):
        return pltpu.make_async_copy(queries[part], q.at[part], q_sems.at[part])

    for part in range(parts):
        query_copy(part).start()

    def queries_of(part, kv_head):
        head = kv_head * heads
        return jnp.concatenate(
            [
                q[part, :, (head + i) * HEAD_SIZE : (head + i + 1) * HEAD_SIZE]
                for i in range(heads)
            ],
            axis=0,
        )

    def lane_tiles(x):
        return [x[:, i : i + HEAD_SIZE] for i in range(0, x.shape[1], HEAD_SIZE)]

    def step(part, kv_head, keys, values, mask, first):
        s = lax.dot_general(
            queries_of(part, kv_head),
            keys,
            (((1,), (1,)), ((), ())),
            preferred_element_type=jnp.float32,
        )
        s = mask(s)
        tops = functools.reduce(jnp.maximum, lane_tiles(s))
        top = jnp.broadcast_to(jnp.max(tops, axis=1, keepdims=True), (rows, HEAD_SIZE))
        if not first:
            before = top_s[kv_head]
            top = jnp.maximum(before, top)
            alpha = jnp.exp2((before - top) * factor)
        weights = [jnp.exp2((tile - top) * factor) for tile in lane_tiles(s)]
        sums = functools.reduce(jnp.add, weights)
        product = lax.dot_general(
            jnp.concatenate([w.astype(jnp.bfloat16) for w in weights], axis=1),
            values,
            (((1,), (0,)), ((), ())),
            preferred_element_type=jnp.float32,
        )
        top_s[kv_head] = top
        if first:
            sum_s[kv_head] = sums
            acc_s[kv_head] = product
        else:
            sum_s[kv_head] = sum_s[kv_head] * alpha + sums
            acc_s[kv_head] = acc_s[kv_head] * alpha + product

    def columns_of(kv_head):
        return slice(kv_head * HEAD_SIZE, (kv_head + 1) * HEAD_SIZE)

    def begin_suffix():
        def causal(s):
            token = lax.broadcasted_iota(jnp.int32, s.shape, 0) % tokens + first_token
            key = lax.broadcasted_iota(jnp.int32, s.shape, 1)
            return jnp.where(key <= token, s, nothing)

        keys = slice(0, first_token + tokens)
        for kv_head in range(kv_heads):
            columns = columns_of(kv_head)
            step(0, kv_head, suffix_kv[0, keys, columns], suffix_kv[1, keys, columns], causal, True)

    def begin_empty():
        top_s[...] = jnp.full(top_s.shape, nothing, jnp.float32)
        sum_s[...] = jnp.zeros(sum_s.shape, jnp.float32)
        acc_s[...] = jnp.zeros(acc_s.shape, jnp.float32)

    def part_step(part, carry):
        base, started = carry
        blocks = blocks_of(part)
        after = jnp.minimum(part + 1, parts - 1)
        more = (part + 1 < parts) & (blocks_of(after) > 0)

        @pl.when((blocks > 0) & jnp.logical_not(started))
        def _():
            start(part, 0, lax.rem(base, 2))

        for i in range(parts):

            @pl.when(part == i)
            def _():
                query_copy(i).wait()

        if suffix:
            pl.when(part == 0)(begin_suffix)
            pl.when(part != 0)(begin_empty)
        else:
            begin_empty()

        def block_step(block, carry):
            slot = lax.rem(base + block, 2)
            last = block + 1 == blocks

            @pl.when(jnp.logical_not(last) | more)
            def _():
                start(jnp.where(last, after, part), jnp.where(last, 0, block + 1), 1 - slot)

            for place in range(pages_per_block):
                copy_of(part, block, slot, place).wait()
            key = lax.broadcasted_iota(jnp.int32, (1, block_keys), 1)
            left = (live_of(part) - block * pages_per_block) * page_tokens
            bias = jnp.where(key < left, 0.0, nothing)
            for kv_head in range(kv_heads):
                keys = buf[slot, :, 0, :, columns_of(kv_head)].reshape(block_keys, HEAD_SIZE)
                values = buf[slot, :, 1, :, columns_of(kv_head)].reshape(block_keys, HEAD_SIZE)
                step(part, kv_head, keys, values, lambda s: s + bias, False)
            return carry

        lax.fori_loop(0, blocks, block_step, 0)

        lane = lax.broadcasted_iota(jnp.int32, (tokens, HEAD_SIZE), 1)
        packed = jnp.zeros((tokens, HEAD_SIZE), jnp.float32)
        for kv_head in range(kv_heads):
            total = jnp.sum(sum_s[kv_head], axis=1, keepdims=True)
            any_key = total > 0.0
            safe = jnp.where(any_key, total, 1.0)
            acc_s[kv_head] = acc_s[kv_head] * (1.0 / safe)
            stat = jnp.where(any_key, top_s[kv_head] * factor + jnp.log2(safe), nothing)
            for i in range(heads):
                packed = jnp.where(
                    lane == kv_head * heads + i, stat[i * tokens : (i + 1) * tokens], packed
                )
        packed = packed.T[: kv_heads * heads]
        for i in range(parts):

            @pl.when(part == i)
            def _():
                lses[i][...] = packed
                for kv_head in range(kv_heads):
                    for j in range(heads):
                        head = kv_head * heads + j
                        outs[i][:, head * HEAD_SIZE : (head + 1) * HEAD_SIZE] = acc_s[
                            kv_head, j * tokens : (j + 1) * tokens
                        ].astype(jnp.bfloat16)

        return base + blocks, (blocks > 0) & more

    lax.fori_loop(0, parts, part_step, (jnp.int32(0), False))


def attend(which, lists, counts, token, queries, pages, first_token=0, suffix=None):
    tokens, width = queries[0].shape
    parts = len(queries)
    page_tokens, kv_width = pages.shape[2:]
    kv_heads = kv_width // HEAD_SIZE
    heads = width // kv_width
    rows = heads * tokens
    vmem = pl.BlockSpec(memory_space=pltpu.VMEM)
    smem = pl.BlockSpec(memory_space=pltpu.SMEM)
    anywhere = pl.BlockSpec(memory_space=pl.ANY)
    extra = () if suffix is None else (suffix,)
    kernel = functools.partial(
        attend_kernel,
        parts=parts,
        kv_heads=kv_heads,
        heads=heads,
        tokens=tokens,
        first_token=first_token,
        suffix=suffix is not None,
    )
    results = pl.pallas_call(
        kernel,
        name="attend_own" if suffix is not None else "attend",
        out_shape=[jax.ShapeDtypeStruct((tokens, width), jnp.bfloat16)] * parts
        + [jax.ShapeDtypeStruct((kv_heads * heads, tokens), jnp.float32)] * parts,
        in_specs=[smem, smem, smem] + [anywhere] * (parts + 2) + [vmem] * len(extra),
        out_specs=[vmem] * (2 * parts),
        scratch_shapes=[
            pltpu.VMEM((parts, tokens, width), jnp.bfloat16),
            pltpu.SemaphoreType.DMA((parts,)),
            pltpu.VMEM((2, pages_per_block, 2, page_tokens, kv_width), jnp.bfloat16),
            pltpu.SemaphoreType.DMA((2, pages_per_block)),
            pltpu.VMEM((kv_heads, rows, HEAD_SIZE), jnp.float32),
            pltpu.VMEM((kv_heads, rows, HEAD_SIZE), jnp.float32),
            pltpu.VMEM((kv_heads, rows, HEAD_SIZE), jnp.float32),
        ],
        cost_estimate=pl.CostEstimate(
            flops=10_000_000_000, bytes_accessed=6_000_000, transcendentals=0
        ),
    )(which, lists, counts, token, *queries, pages, *extra)
    return list(zip(results[:parts], results[parts:]))


def combine_kernel(token, *refs, parts, heads):
    outs, lses = refs[:parts], refs[parts : 2 * parts]
    out, lse = refs[2 * parts :]
    tokens = out.shape[0]
    blank = jnp.full((HEAD_SIZE - heads, tokens), nothing, jnp.float32)
    stats = [jnp.concatenate([x[...], blank], axis=0).T for x in lses]
    top = functools.reduce(jnp.maximum, stats)
    shares = [jnp.exp2(x - top) for x in stats]
    total = functools.reduce(jnp.add, shares)
    shares = [x / total for x in shares]
    lse[...] = (top + jnp.log2(total)).T[:heads]
    for head in range(heads):
        columns = slice(head * HEAD_SIZE, (head + 1) * HEAD_SIZE)
        terms = [
            o[:, columns].astype(jnp.float32) * share[:, head : head + 1]
            for o, share in zip(outs, shares)
        ]
        out[:, columns] = functools.reduce(jnp.add, terms).astype(jnp.bfloat16)


def combine(parts, token):
    tokens, width = parts[0][0].shape
    heads = width // HEAD_SIZE
    vmem = pl.BlockSpec(memory_space=pltpu.VMEM)
    return pl.pallas_call(
        functools.partial(combine_kernel, parts=len(parts), heads=heads),
        name="combine",
        out_shape=(
            jax.ShapeDtypeStruct((tokens, width), jnp.bfloat16),
            jax.ShapeDtypeStruct((heads, tokens), jnp.float32),
        ),
        in_specs=[pl.BlockSpec(memory_space=pl.ANY)] + [vmem] * (2 * len(parts)),
        out_specs=(vmem, vmem),
        cost_estimate=pl.CostEstimate(
            flops=1_000_000_000, bytes_accessed=3_000_000, transcendentals=0
        ),
    )(token, *[p[0] for p in parts], *[p[1] for p in parts])


def page_lists(page_ids, prefix_pages, page_home, pool_rows):
    cache_index = lax.axis_index("cache")
    slots = page_ids.shape[1]
    sent = jnp.concatenate([page_ids, prefix_pages[:, None]], axis=1)
    arrived = lax.all_gather(sent, "cache", axis=0, tiled=True)
    ids, lengths = arrived[:, :slots], arrived[:, slots]
    table = jnp.arange(page_home.shape[0], dtype=jnp.int32)
    rows = jnp.sum(jnp.where(ids[:, :, None] == table, page_home, 0), axis=2)
    within = rows - cache_index * pool_rows
    slot = jnp.arange(slots, dtype=jnp.int32)
    mine = (within >= 0) & (within < pool_rows) & (slot[None, :] < lengths[:, None])
    earlier = slot[:, None] < slot[None, :]
    rank = jnp.sum(jnp.where(earlier[None] & mine[:, :, None], 1, 0), axis=1)
    chosen = mine[:, :, None] & (rank[:, :, None] == slot)
    lists = jnp.sum(jnp.where(chosen, within[:, :, None], 0), axis=1)
    return lists.astype(jnp.int32), jnp.sum(mine, axis=1).astype(jnp.int32)


def place_kernel(source, *refs):
    terms, out = refs[:-1], refs[-1]
    for i, term in enumerate(terms):
        out[source[i]] = term[...]


def place(sources, terms):
    tokens, width = terms[0].shape
    vmem = pl.BlockSpec(memory_space=pltpu.VMEM)
    return pl.pallas_call(
        place_kernel,
        name="place",
        out_shape=jax.ShapeDtypeStruct((len(terms), tokens, width), terms[0].dtype),
        in_specs=[pl.BlockSpec(memory_space=pltpu.SMEM)] + [vmem] * len(terms),
        out_specs=vmem,
    )(jnp.stack(sources), *terms)


def reduce_line(terms, out_blocks):
    count = lax.axis_size("tensor")
    z = lax.axis_index("tensor")

    def chunk(index):
        index = jnp.clip(index, 0, count - 1)
        return lax.dynamic_slice_in_dim(terms, index * out_blocks, out_blocks, 0)

    def add(*parts):
        return functools.reduce(jnp.add, [p.astype(jnp.float32) for p in parts]).astype(terms.dtype)

    up = down = None
    for step in range(1, count):
        up_send, down_send = chunk(count - step + z), chunk(z - (count - step))
        if up is not None:
            up_send, down_send = add(up_send, up), add(down_send, down)
        up = lax.ppermute(up_send, "tensor", [(i, i + 1) for i in range(step)])
        down = lax.ppermute(
            down_send, "tensor", [(count - 1 - i, count - 2 - i) for i in range(step)]
        )
    return add(chunk(z), up, down)


def attention_block(queries, suffix_key_value, kv_pages, page_ids, prefix_pages, page_home, out_weight):
    cache_count = lax.axis_size("cache")
    cache_index = lax.axis_index("cache")
    pool_rows = kv_pages.shape[0]
    chips = cache_count // 2
    chip, core = cache_index // 2, cache_index % 2
    tokens = queries.shape[0] // token_pieces

    def swap(x, chip_shift, other_core):
        pairs = []
        for source in range(cache_count):
            at_chip, at_core = source // 2, source % 2
            at_core = 1 - at_core if other_core else at_core
            pairs.append((source, (at_chip + chip_shift) % chips * 2 + at_core))
        return jax.tree.map(lambda leaf: lax.ppermute(leaf, "cache", pairs), x)

    def device_at(chip_shift, other_core):
        return (chip + chip_shift) % chips * 2 + (1 - core if other_core else core)

    lists, counts = page_lists(page_ids, prefix_pages, page_home, pool_rows)
    queries, lists = lax.optimization_barrier((queries, lists))
    pieces = [queries[i * tokens : (i + 1) * tokens] for i in range(token_pieces)]
    near = [[piece] + [swap(piece, s, False) for s in range(1, chips)] for piece in pieces]

    def attend_pair(piece, s, same, token):
        which = jnp.stack([device_at(-s, False), device_at(-s, True)])
        pair = [same, swap(same, 0, True)]
        return attend(
            which,
            lists,
            counts,
            token,
            pair,
            kv_pages,
            piece * tokens,
            None if s else suffix_key_value,
        )

    def attend_far(piece, token):
        joined = []
        for s, same in enumerate(near[piece][1:], 1):
            mine, theirs = attend_pair(piece, s, same, token)
            theirs = swap(theirs, 0, True)
            joined.append(combine([mine, theirs], token))
        sent = [swap(x, -s, False) for s, x in enumerate(joined, 1)]
        return sent, joined[-1][1]

    def mix(piece, token):
        mine, theirs = own[piece]
        theirs = swap(theirs, 0, True)
        return combine([mine, theirs, *far[piece]], token)

    def terms_of(piece, s):
        block = swap(mixed[piece], s, False) if s else mixed[piece]
        results = []
        for other in (False, True):
            here = swap(block, 0, True) if other else block
            term = jnp.dot(here, out_weight, preferred_element_type=jnp.float32)
            term = term.astype(jnp.bfloat16)
            results.append(swap(term, -s, other) if s or other else term)
        return results

    def reduce_terms(terms):
        sources = [device_at(s, other) for s in range(chips) for other in (False, True)]
        placed = place(sources, terms)
        summed = reduce_line(placed, cache_count // lax.axis_size("tensor"))
        return jnp.concatenate([summed[i] for i in range(summed.shape[0])], axis=1)

    own, far, mixed = {}, {}, {}
    own[0] = attend_pair(0, 0, near[0][0], counts)
    near[0][1:], own[0] = lax.optimization_barrier((near[0][1:], own[0]))
    token = own[0][0][1]
    for piece in range(token_pieces):
        far[piece], token = attend_far(piece, token)
    for piece in range(token_pieces):
        if piece:
            own[piece] = attend_pair(piece, 0, near[piece][0], token)
            token = own[piece][0][1]
        mixed[piece], token = mix(piece, token)
    results = [
        reduce_terms([term for s in range(chips) for term in terms_of(piece, s)])
        for piece in range(token_pieces)
    ]
    return jnp.concatenate(results, axis=0)


def solution(mesh):
    in_specs = (
        P(("groups", "cache"), "tensor"),
        P(None, ("groups", "cache"), "tensor"),
        P(("groups", "cache"), None, None, "tensor"),
        P(("groups", "cache"), None),
        P(("groups", "cache")),
        P("groups"),
        P("tensor", "cache"),
    )
    out_specs = P(("groups", "cache"), "tensor")
    return jax.shard_map(
        attention_block, mesh=mesh, in_specs=in_specs, out_specs=out_specs, check_vma=False
    )
```

time: 629 us -> 304 us (0.48)
  the two profiles are of different devices: /device:TPU:0 before, /device:TPU:12 now
where the time goes in v1:
time: 304 us; the launch traced here: 303 us
  waiting for transfers between devices  95.6 us (31%)
  Pallas kernels  81.2 us (27%)
  starting transfers between devices  61.8 us (20%)
  matrix products  24.6 us (8%)
  other arithmetic  19.9 us (7%)
  local copies, waits for them, and re-layouts  13.6 us (4%)
  blocking collectives  5.05 us (2%)
    pallas_call x4, Pallas kernels, attend(): pl.pallas_call(kernel, name='attend_own' if suffix is not None else 'atte...  63.1 us
    ppermute x30, waiting for transfers between devices, swap(): return jax.tree.map(lambda leaf: lax.ppermute(leaf, 'cache', pairs), x)  50.1 us
    ppermute x30, starting transfers between devices, swap(): return jax.tree.map(lambda leaf: lax.ppermute(leaf, 'cache', pairs), x)  36.7 us
    dot_general x8, matrix products, terms_of(): term = jnp.dot(here, out_weight, preferred_element_type=jnp.float32)  24.6 us
    ppermute x6, waiting for transfers between devices, reduce_line(): up = lax.ppermute(up_send, 'tensor', [(i, i + 1) for i in range(step)])  24.5 us
    ppermute x6, waiting for transfers between devices, reduce_line(): lax.ppermute(down_send, 'tensor', [(count - 1 - i, count - 2 - i) for i i...  21 us
    ppermute x6, starting transfers between devices, reduce_line(): up = lax.ppermute(up_send, 'tensor', [(i, i + 1) for i in range(step)])  15.7 us
    pallas_call x4, Pallas kernels, combine(): pl.pallas_call(functools.partial(combine_kernel, parts=len(parts), heads=...  12 us
  transfers between devices with their start and end apart: 42, of which 17 were waited for; matrix products, arithmetic and copies ran while one was open for 14% of the time, Pallas kernels for 24%

profile of v1, /device:TPU:12, one launch (start us, length us, event | category | flops | bytes accessed | tf_op | source)
XLA Modules:
  0.0 303.0 jit_solution(14968088132084506016)
XLA Ops:
  1.4 5.0 %all-gather = s32[4,1,65]{2,1,0:T(1,128)S(1)} all-gather(s32[1,1,65]{2,1,0:T(1,128)S(1)} %add_bitcast_fusion), channel_id=1, replica_groups=mesh['groups'=2,'cache'=4,'tensor'=4] {'cache'}, dimensions={0}, use_global_device_ids=true | all-gather | bytes 1300 | tf_op jit(solution)/shard_map/all_gather | solution.py:272
  13.7 22.0 %attend_own.2 = (bf16[128,2048]{1,0:T(8,128)(2,1)}, bf16[128,2048]{1,0:T(8,128)(2,1)}, f32[16,128]{1,0:T(8,128)}, f32[16,128]{1,0:T(8,128)}) custom-call(s32[2]{0:T(128)} %pad_add_fusion.1.which, s32[4,64]{1,0:T(4,128)} %select_reduce_fusion.1.lists, s32[4]{0:T(128)} %get-tuple-element.65.counts.token, s32[4]{0:T(128)} %get-tuple-element.65.counts.token, ...), custom_call_target="tpu_custom_call" | custom-call | flops 10000000000 | bytes 6000000 | tf_op jit(solution)/shard_map/attend_own/pallas_call | solution.py:206
  38.5 9.4 %attend.2 = (bf16[128,2048]{1,0:T(8,128)(2,1)}, bf16[128,2048]{1,0:T(8,128)(2,1)}, f32[16,128]{1,0:T(8,128)}, f32[16,128]{1,0:T(8,128)}) custom-call(s32[2]{0:T(128)} %pad_add_fusion.2.which, s32[4,64]{1,0:T(4,128)} %select_reduce_fusion.1.lists, s32[4]{0:T(128)} %get-tuple-element.65.counts.token, f32[16,128]{1,0:T(8,128)} %get-tuple-element.41.token.refs_3_, ...), custom_call_target="tpu_custom_call" | custom-call | flops 10000000000 | bytes 6000000 | tf_op jit(solution)/shard_map/attend/pallas_call | solution.py:206
  47.9 3.7 %collective-permute-start.3 = (bf16[128,2048]{1,0:T(8,128)(2,1)}, bf16[128,2048]{1,0:T(8,128)(2,1)S(1)}, u32[]{:S(2)}, u32[]{:S(2)}) collective-permute-start(bf16[128,2048]{1,0:T(8,128)(2,1)} %get-tuple-element.44), channel_id=1, source_target_pairs={{0,4},{4,0},{8,12},{12,8},{1,5},{5,1},{9,13},{13,9},{2,6},{6,2},{1... | collective-permute-start | bytes 1572872 | tf_op jit(solution)/shard_map/ppermute | solution.py:341
  58.5 9.5 %attend.3 = (bf16[128,2048]{1,0:T(8,128)(2,1)}, bf16[128,2048]{1,0:T(8,128)(2,1)}, f32[16,128]{1,0:T(8,128)}, f32[16,128]{1,0:T(8,128)}) custom-call(s32[2]{0:T(128)} %pad_add_fusion.2.which, s32[4,64]{1,0:T(4,128)} %select_reduce_fusion.1.lists, s32[4]{0:T(128)} %get-tuple-element.65.counts.token, f32[16,128]{1,0:T(8,128)} %get-tuple-element.47.token, ...), custom_call_target="tpu_custom_call" | custom-call | flops 10000000000 | bytes 6000000 | tf_op jit(solution)/shard_map/attend/pallas_call | solution.py:206
  68.0 3.9 %collective-permute-start.7 = (bf16[128,2048]{1,0:T(8,128)(2,1)}, bf16[128,2048]{1,0:T(8,128)(2,1)}, u32[]{:S(2)}, u32[]{:S(2)}) collective-permute-start(bf16[128,2048]{1,0:T(8,128)(2,1)} %get-tuple-element.49), channel_id=1, source_target_pairs={{0,4},{4,0},{8,12},{12,8},{1,5},{5,1},{9,13},{13,9},{2,6},{6,2},{1... | collective-permute-start | bytes 1572872 | tf_op jit(solution)/shard_map/ppermute | solution.py:341
  72.1 17.4 %collective-permute-start.10 = (bf16[128,2048]{1,0:T(8,128)(2,1)S(1)}, bf16[128,2048]{1,0:T(8,128)(2,1)S(1)}, u32[]{:S(2)}, u32[]{:S(2)}) collective-permute-start(bf16[128,2048]{1,0:T(8,128)(2,1)S(1)} %copy-done.11), channel_id=1, source_target_pairs={{0,8},{4,12},{8,0},{12,4},{1,9},{5,13},{9,1},{13,5},{2,10},{6,14},... | collective-permute-start | bytes 1572872 | tf_op jit(solution)/shard_map/ppermute | solution.py:341
  96.4 5.8 %collective-permute-done.12.refs_5_ = f32[16,128]{1,0:T(8,128)S(1)} collective-permute-done((f32[16,128]{1,0:T(8,128)S(1)}, f32[16,128]{1,0:T(8,128)S(1)}, u32[]{:S(2)}, u32[]{:S(2)}) %collective-permute-start.12) | collective-permute-done | bytes 8224 | tf_op jit(solution)/shard_map/ppermute | solution.py:341
  107.8 22.2 %attend_own.3 = (bf16[128,2048]{1,0:T(8,128)(2,1)}, bf16[128,2048]{1,0:T(8,128)(2,1)}, f32[16,128]{1,0:T(8,128)}, f32[16,128]{1,0:T(8,128)}) custom-call(s32[2]{0:T(128)} %pad_add_fusion.1.which, s32[4,64]{1,0:T(4,128)} %select_reduce_fusion.1.lists, s32[4]{0:T(128)} %get-tuple-element.65.counts.token, f32[16,128]{1,0:T(8,128)} %get-tuple-element.58.token, ...), custom_call_target="tpu_custom_call" | custom-call | flops 10000000000 | bytes 6000000 | tf_op jit(solution)/shard_map/attend_own/pallas_call | solution.py:206
  130.7 5.5 %convolution_convert_fusion.7.refs_0_ = bf16[128,2048]{1,0:T(8,128)(2,1)} fusion(bf16[128,2048]{1,0:T(8,128)(2,1)S(1)} %copy-done.2, bf16[2048,2048]{1,0:T(8,128)(2,1)} %param.13), kind=kOutput, calls=%fused_computation.7 | convolution fusion | flops 1074003968 | bytes 9437184 | tf_op jit(solution)/shard_map/dot_general | solution.py:384
  138.1 6.8 %collective-permute-done.27.refs_2_ = bf16[128,2048]{1,0:T(8,128)(2,1)S(1)} collective-permute-done((bf16[128,2048]{1,0:T(8,128)(2,1)S(1)}, bf16[128,2048]{1,0:T(8,128)(2,1)S(1)}, u32[]{:S(2)}, u32[]{:S(2)}) %collective-permute-start.27) | collective-permute-done | bytes 524320 | tf_op jit(solution)/shard_map/ppermute | solution.py:341
  149.1 4.8 %convolution_convert_fusion.6 = bf16[128,2048]{1,0:T(8,128)(2,1)S(1)} fusion(bf16[128,2048]{1,0:T(8,128)(2,1)S(1)} %collective-permute-done.13, bf16[2048,2048]{1,0:T(8,128)(2,1)} %param.13), kind=kOutput, calls=%fused_computation.6 | convolution fusion | flops 1074003968 | bytes 9437184 | tf_op jit(solution)/shard_map/dot_general | solution.py:384
  160.2 7.1 %collective-permute-done.32 = bf16[128,2048]{1,0:T(8,128)(2,1)S(1)} collective-permute-done((bf16[128,2048]{1,0:T(8,128)(2,1)}, bf16[128,2048]{1,0:T(8,128)(2,1)S(1)}, u32[]{:S(2)}, u32[]{:S(2)}) %collective-permute-start.32) | collective-permute-done | bytes 524320 | tf_op jit(solution)/shard_map/ppermute | solution.py:341
  175.3 3.3 %collective-permute-done.16.refs_2_ = bf16[128,2048]{1,0:T(8,128)(2,1)S(1)} collective-permute-done((bf16[128,2048]{1,0:T(8,128)(2,1)S(1)}, bf16[128,2048]{1,0:T(8,128)(2,1)S(1)}, u32[]{:S(2)}, u32[]{:S(2)}) %collective-permute-start.16) | collective-permute-done | bytes 524320 | tf_op jit(solution)/shard_map/ppermute | solution.py:341
  178.6 21.4 %collective-permute-done.18.refs_3_ = bf16[128,2048]{1,0:T(8,128)(2,1)S(1)} collective-permute-done((bf16[128,2048]{1,0:T(8,128)(2,1)S(1)}, bf16[128,2048]{1,0:T(8,128)(2,1)S(1)}, u32[]{:S(2)}, u32[]{:S(2)}) %collective-permute-start.18) | collective-permute-done | bytes 524320 | tf_op jit(solution)/shard_map/ppermute | solution.py:341
  207.8 5.4 %convolution_convert_fusion.3.refs_0_ = bf16[128,2048]{1,0:T(8,128)(2,1)} fusion(bf16[128,2048]{1,0:T(8,128)(2,1)S(1)} %copy-done.1, bf16[2048,2048]{1,0:T(8,128)(2,1)} %param.13), kind=kOutput, calls=%fused_computation.3 | convolution fusion | flops 1074003968 | bytes 9437184 | tf_op jit(solution)/shard_map/dot_general | solution.py:384
  227.9 8.2 %collective-permute-done.36 = bf16[1,128,2048]{2,1,0:T(8,128)(2,1)} collective-permute-done((bf16[1,128,2048]{2,1,0:T(8,128)(2,1)S(1)}, bf16[1,128,2048]{2,1,0:T(8,128)(2,1)}, u32[]{:S(2)}, u32[]{:S(2)}) %collective-permute-start.36) | collective-permute-done | bytes 524320 | tf_op jit(solution)/shard_map/ppermute | solution.py:320
  239.4 8.0 %collective-permute-done.20 = bf16[1,128,2048]{2,1,0:T(8,128)(2,1)} collective-permute-done((bf16[1,128,2048]{2,1,0:T(8,128)(2,1)S(1)}, bf16[1,128,2048]{2,1,0:T(8,128)(2,1)}, u32[]{:S(2)}, u32[]{:S(2)}) %collective-permute-start.20) | collective-permute-done | bytes 524320 | tf_op jit(solution)/shard_map/ppermute | solution.py:320
  251.2 7.4 %collective-permute-done.37 = bf16[1,128,2048]{2,1,0:T(8,128)(2,1)} collective-permute-done((bf16[1,128,2048]{2,1,0:T(8,128)(2,1)S(1)}, bf16[1,128,2048]{2,1,0:T(8,128)(2,1)}, u32[]{:S(2)}, u32[]{:S(2)}) %collective-permute-start.37) | collective-permute-done | bytes 524320 | tf_op jit(solution)/shard_map/ppermute | solution.py:320
  262.7 4.6 %collective-permute-start.21 = (bf16[1,128,2048]{2,1,0:T(8,128)(2,1)}, bf16[1,128,2048]{2,1,0:T(8,128)(2,1)S(1)}, u32[]{:S(2)}, u32[]{:S(2)}) collective-permute-start(bf16[1,128,2048]{2,1,0:T(8,128)(2,1)} %get-tuple-element.68), channel_id=1, source_target_pairs={{0,1},{1,2},{2,3},{4,5},{5,6},{6,7},{8,9},{9,10},{10,11},{12,13},{... | collective-permute-start | bytes 1572872 | tf_op jit(solution)/shard_map/ppermute | solution.py:320
  270.2 3.9 %collective-permute-start.38 = (bf16[1,128,2048]{2,1,0:T(8,128)(2,1)}, bf16[1,128,2048]{2,1,0:T(8,128)(2,1)S(1)}, u32[]{:S(2)}, u32[]{:S(2)}) collective-permute-start(bf16[1,128,2048]{2,1,0:T(8,128)(2,1)} %get-tuple-element.72), channel_id=1, source_target_pairs={{0,1},{1,2},{2,3},{4,5},{5,6},{6,7},{8,9},{9,10},{10,11},{12,13},{... | collective-permute-start | bytes 1572872 | tf_op jit(solution)/shard_map/ppermute | solution.py:320
  274.1 4.4 %collective-permute-done.40 = bf16[1,128,2048]{2,1,0:T(8,128)(2,1)} collective-permute-done((bf16[1,128,2048]{2,1,0:T(8,128)(2,1)}, bf16[1,128,2048]{2,1,0:T(8,128)(2,1)}, u32[]{:S(2)}, u32[]{:S(2)}) %collective-permute-start.40) | collective-permute-done | bytes 524320 | tf_op jit(solution)/shard_map/ppermute | solution.py:321
  282.5 7.2 %collective-permute-done.24 = bf16[1,128,2048]{2,1,0:T(8,128)(2,1)} collective-permute-done((bf16[1,128,2048]{2,1,0:T(8,128)(2,1)}, bf16[1,128,2048]{2,1,0:T(8,128)(2,1)}, u32[]{:S(2)}, u32[]{:S(2)}) %collective-permute-start.24) | collective-permute-done | bytes 524320 | tf_op jit(solution)/shard_map/ppermute | solution.py:321
  291.0 9.5 %collective-permute-done.41 = bf16[1,128,2048]{2,1,0:T(8,128)(2,1)} collective-permute-done((bf16[1,128,2048]{2,1,0:T(8,128)(2,1)}, bf16[1,128,2048]{2,1,0:T(8,128)(2,1)}, u32[]{:S(2)}, u32[]{:S(2)}) %collective-permute-start.41) | collective-permute-done | bytes 524320 | tf_op jit(solution)/shard_map/ppermute | solution.py:321
  (168 shorter events, 95.4 us)
Async XLA Ops:
  10.8 24.9 %collective-permute-start = (bf16[128,2048]{1,0:T(8,128)(2,1)S(1)}, bf16[128,2048]{1,0:T(8,128)(2,1)S(1)}, u32[]{:S(2)}, u32[]{:S(2)}) collective-permute-start(bf16[128,2048]{1,0:T(8,128)(2,1)S(1)} %get-tuple-element.77.refs_0_), channel_id=1, source_target_pairs={{0,8},{4,12},{8,0},{12,4},{1,9},{5,13},{9,1},{13,5},{2,10},{6,14},... | collective-permute-start | bytes 1572872 | tf_op jit(solution)/shard_map/ppermute | solution.py:341
  68.0 23.6 %collective-permute-start.7 = (bf16[128,2048]{1,0:T(8,128)(2,1)}, bf16[128,2048]{1,0:T(8,128)(2,1)}, u32[]{:S(2)}, u32[]{:S(2)}) collective-permute-start(bf16[128,2048]{1,0:T(8,128)(2,1)} %get-tuple-element.49), channel_id=1, source_target_pairs={{0,4},{4,0},{8,12},{12,8},{1,5},{5,1},{9,13},{13,9},{2,6},{6,2},{1... | collective-permute-start | bytes 1572872 | tf_op jit(solution)/shard_map/ppermute | solution.py:341
  72.0 24.5 %collective-permute-start.9 = (bf16[128,2048]{1,0:T(8,128)(2,1)S(1)}, bf16[128,2048]{1,0:T(8,128)(2,1)S(1)}, u32[]{:S(2)}, u32[]{:S(2)}) collective-permute-start(bf16[128,2048]{1,0:T(8,128)(2,1)S(1)} %copy-done.9), channel_id=1, source_target_pairs={{0,4},{4,0},{8,12},{12,8},{1,5},{5,1},{9,13},{13,9},{2,6},{6,2},{1... | collective-permute-start | bytes 1572872 | tf_op jit(solution)/shard_map/ppermute | solution.py:341
  72.1 30.2 %collective-permute-start.10 = (bf16[128,2048]{1,0:T(8,128)(2,1)S(1)}, bf16[128,2048]{1,0:T(8,128)(2,1)S(1)}, u32[]{:S(2)}, u32[]{:S(2)}) collective-permute-start(bf16[128,2048]{1,0:T(8,128)(2,1)S(1)} %copy-done.11), channel_id=1, source_target_pairs={{0,8},{4,12},{8,0},{12,4},{1,9},{5,13},{9,1},{13,5},{2,10},{6,14},... | collective-permute-start | bytes 1572872 | tf_op jit(solution)/shard_map/ppermute | solution.py:341
  89.5 17.4 %collective-permute-start.25 = (bf16[128,2048]{1,0:T(8,128)(2,1)S(1)}, bf16[128,2048]{1,0:T(8,128)(2,1)S(1)}, u32[]{:S(2)}, u32[]{:S(2)}) collective-permute-start(bf16[128,2048]{1,0:T(8,128)(2,1)S(1)} %get-tuple-element.76.refs_0_), channel_id=1, source_target_pairs={{0,4},{4,0},{8,12},{12,8},{1,5},{5,1},{9,13},{13,9},{2,6},{6,2},{1... | collective-permute-start | bytes 1572872 | tf_op jit(solution)/shard_map/ppermute | solution.py:341
  95.8 42.3 %collective-permute-start.29 = (f32[16,128]{1,0:T(8,128)}, f32[16,128]{1,0:T(8,128)S(1)}, u32[]{:S(2)}, u32[]{:S(2)}) collective-permute-start(f32[16,128]{1,0:T(8,128)} %get-tuple-element.52.token), channel_id=1, source_target_pairs={{0,8},{4,12},{8,0},{12,4},{1,9},{5,13},{9,1},{13,5},{2,10},{6,14},... | collective-permute-start | bytes 24584 | tf_op jit(solution)/shard_map/ppermute | solution.py:341
  130.5 18.6 %collective-permute-start.13 = (bf16[128,2048]{1,0:T(8,128)(2,1)S(1)}, bf16[128,2048]{1,0:T(8,128)(2,1)S(1)}, u32[]{:S(2)}, u32[]{:S(2)}) collective-permute-start(bf16[128,2048]{1,0:T(8,128)(2,1)S(1)} %copy-done.2), channel_id=1, source_target_pairs={{0,4},{4,0},{8,12},{12,8},{1,5},{5,1},{9,13},{13,9},{2,6},{6,2},{1... | collective-permute-start | bytes 1572872 | tf_op jit(solution)/shard_map/ppermute | solution.py:341
  136.1 20.0 %collective-permute-start.15 = (bf16[128,2048]{1,0:T(8,128)(2,1)S(1)}, bf16[128,2048]{1,0:T(8,128)(2,1)S(1)}, u32[]{:S(2)}, u32[]{:S(2)}) collective-permute-start(bf16[128,2048]{1,0:T(8,128)(2,1)S(1)} %copy-done.2), channel_id=1, source_target_pairs={{0,8},{4,12},{8,0},{12,4},{1,9},{5,13},{9,1},{13,5},{2,10},{6,14},... | collective-permute-start | bytes 1572872 | tf_op jit(solution)/shard_map/ppermute | solution.py:341
  149.0 18.3 %collective-permute-start.32 = (bf16[128,2048]{1,0:T(8,128)(2,1)}, bf16[128,2048]{1,0:T(8,128)(2,1)S(1)}, u32[]{:S(2)}, u32[]{:S(2)}) collective-permute-start(bf16[128,2048]{1,0:T(8,128)(2,1)} %get-tuple-element.64), channel_id=1, source_target_pairs={{0,8},{4,12},{8,0},{12,4},{1,9},{5,13},{9,1},{13,5},{2,10},{6,14},... | collective-permute-start | bytes 1572872 | tf_op jit(solution)/shard_map/ppermute | solution.py:341
  153.9 21.3 %collective-permute-start.14 = (bf16[128,2048]{1,0:T(8,128)(2,1)S(1)}, bf16[128,2048]{1,0:T(8,128)(2,1)S(1)}, u32[]{:S(2)}, u32[]{:S(2)}) collective-permute-start(bf16[128,2048]{1,0:T(8,128)(2,1)S(1)} %convolution_convert_fusion.6), channel_id=1, source_target_pairs={{0,4},{4,0},{8,12},{12,8},{1,5},{5,1},{9,13},{13,9},{2,6},{6,2},{1... | collective-permute-start | bytes 1572872 | tf_op jit(solution)/shard_map/ppermute | solution.py:341
  157.5 21.1 %collective-permute-start.16 = (bf16[128,2048]{1,0:T(8,128)(2,1)S(1)}, bf16[128,2048]{1,0:T(8,128)(2,1)S(1)}, u32[]{:S(2)}, u32[]{:S(2)}) collective-permute-start(bf16[128,2048]{1,0:T(8,128)(2,1)S(1)} %convolution_convert_fusion.5), channel_id=1, source_target_pairs={{0,8},{4,12},{8,0},{12,4},{1,9},{5,13},{9,1},{13,5},{2,10},{6,14},... | collective-permute-start | bytes 1572872 | tf_op jit(solution)/shard_map/ppermute | solution.py:341
  159.9 53.3 %collective-permute-start.31 = (bf16[128,2048]{1,0:T(8,128)(2,1)}, bf16[128,2048]{1,0:T(8,128)(2,1)S(1)}, u32[]{:S(2)}, u32[]{:S(2)}) collective-permute-start(bf16[128,2048]{1,0:T(8,128)(2,1)} %convolution_convert_fusion.2), channel_id=1, source_target_pairs={{0,4},{4,0},{8,12},{12,8},{1,5},{5,1},{9,13},{13,9},{2,6},{6,2},{1... | collective-permute-start | bytes 1572872 | tf_op jit(solution)/shard_map/ppermute | solution.py:341
  169.5 43.7 %collective-permute-start.33 = (bf16[128,2048]{1,0:T(8,128)(2,1)}, bf16[128,2048]{1,0:T(8,128)(2,1)}, u32[]{:S(2)}, u32[]{:S(2)}) collective-permute-start(bf16[128,2048]{1,0:T(8,128)(2,1)} %convolution_convert_fusion.1), channel_id=1, source_target_pairs={{0,8},{4,12},{8,0},{12,4},{1,9},{5,13},{9,1},{13,5},{2,10},{6,14},... | collective-permute-start | bytes 1572872 | tf_op jit(solution)/shard_map/ppermute | solution.py:341
  171.4 28.6 %collective-permute-start.18 = (bf16[128,2048]{1,0:T(8,128)(2,1)S(1)}, bf16[128,2048]{1,0:T(8,128)(2,1)S(1)}, u32[]{:S(2)}, u32[]{:S(2)}) collective-permute-start(bf16[128,2048]{1,0:T(8,128)(2,1)S(1)} %convolution_convert_fusion.4), channel_id=1, source_target_pairs={{0,12},{4,8},{8,4},{12,0},{1,13},{5,9},{9,5},{13,1},{2,14},{6,10},... | collective-permute-start | bytes 1572872 | tf_op jit(solution)/shard_map/ppermute | solution.py:341
  175.3 37.9 %collective-permute-start.35 = (bf16[128,2048]{1,0:T(8,128)(2,1)}, bf16[128,2048]{1,0:T(8,128)(2,1)}, u32[]{:S(2)}, u32[]{:S(2)}) collective-permute-start(bf16[128,2048]{1,0:T(8,128)(2,1)} %convolution_convert_fusion), channel_id=1, source_target_pairs={{0,12},{4,8},{8,4},{12,0},{1,13},{5,9},{9,5},{13,1},{2,14},{6,10},... | collective-permute-start | bytes 1572872 | tf_op jit(solution)/shard_map/ppermute | solution.py:341
  220.4 19.0 %collective-permute-start.22 = (bf16[1,128,2048]{2,1,0:T(8,128)(2,1)}, bf16[1,128,2048]{2,1,0:T(8,128)(2,1)}, u32[]{:S(2)}, u32[]{:S(2)}) collective-permute-start(bf16[1,128,2048]{2,1,0:T(8,128)(2,1)} %get-tuple-element.71), channel_id=1, source_target_pairs={{3,2},{7,6},{11,10},{15,14},{19,18},{23,22},{27,26},{31,30}} | collective-permute-start | bytes 1572872 | tf_op jit(solution)/shard_map/ppermute | solution.py:321
  224.1 23.3 %collective-permute-start.20 = (bf16[1,128,2048]{2,1,0:T(8,128)(2,1)S(1)}, bf16[1,128,2048]{2,1,0:T(8,128)(2,1)}, u32[]{:S(2)}, u32[]{:S(2)}) collective-permute-start(bf16[1,128,2048]{2,1,0:T(8,128)(2,1)S(1)} %add_convert_fusion.9), channel_id=1, source_target_pairs={{0,1},{1,2},{4,5},{5,6},{8,9},{9,10},{12,13},{13,14},{16,17},{17,1... | collective-permute-start | bytes 1572872 | tf_op jit(solution)/shard_map/ppermute | solution.py:320
  226.5 24.7 %collective-permute-start.39 = (bf16[1,128,2048]{2,1,0:T(8,128)(2,1)}, bf16[1,128,2048]{2,1,0:T(8,128)(2,1)}, u32[]{:S(2)}, u32[]{:S(2)}) collective-permute-start(bf16[1,128,2048]{2,1,0:T(8,128)(2,1)} %get-tuple-element.75), channel_id=1, source_target_pairs={{3,2},{7,6},{11,10},{15,14},{19,18},{23,22},{27,26},{31,30}} | collective-permute-start | bytes 1572872 | tf_op jit(solution)/shard_map/ppermute | solution.py:321
  237.4 21.1 %collective-permute-start.37 = (bf16[1,128,2048]{2,1,0:T(8,128)(2,1)S(1)}, bf16[1,128,2048]{2,1,0:T(8,128)(2,1)}, u32[]{:S(2)}, u32[]{:S(2)}) collective-permute-start(bf16[1,128,2048]{2,1,0:T(8,128)(2,1)S(1)} %add_convert_fusion.4), channel_id=1, source_target_pairs={{0,1},{1,2},{4,5},{5,6},{8,9},{9,10},{12,13},{13,14},{16,17},{17,1... | collective-permute-start | bytes 1572872 | tf_op jit(solution)/shard_map/ppermute | solution.py:320
  249.9 17.4 %collective-permute-start.23 = (bf16[1,128,2048]{2,1,0:T(8,128)(2,1)}, bf16[1,128,2048]{2,1,0:T(8,128)(2,1)S(1)}, u32[]{:S(2)}, u32[]{:S(2)}) collective-permute-start(bf16[1,128,2048]{2,1,0:T(8,128)(2,1)} %get-tuple-element.69), channel_id=1, source_target_pairs={{3,2},{2,1},{7,6},{6,5},{11,10},{10,9},{15,14},{14,13},{19,18},{18... | collective-permute-start | bytes 1572872 | tf_op jit(solution)/shard_map/ppermute | solution.py:321
  262.7 19.7 %collective-permute-start.21 = (bf16[1,128,2048]{2,1,0:T(8,128)(2,1)}, bf16[1,128,2048]{2,1,0:T(8,128)(2,1)S(1)}, u32[]{:S(2)}, u32[]{:S(2)}) collective-permute-start(bf16[1,128,2048]{2,1,0:T(8,128)(2,1)} %get-tuple-element.68), channel_id=1, source_target_pairs={{0,1},{1,2},{2,3},{4,5},{5,6},{6,7},{8,9},{9,10},{10,11},{12,13},{... | collective-permute-start | bytes 1572872 | tf_op jit(solution)/shard_map/ppermute | solution.py:320
  268.2 21.4 %collective-permute-start.24 = (bf16[1,128,2048]{2,1,0:T(8,128)(2,1)}, bf16[1,128,2048]{2,1,0:T(8,128)(2,1)}, u32[]{:S(2)}, u32[]{:S(2)}) collective-permute-start(bf16[1,128,2048]{2,1,0:T(8,128)(2,1)} %add_convert_fusion.6), channel_id=1, source_target_pairs={{3,2},{2,1},{1,0},{7,6},{6,5},{5,4},{11,10},{10,9},{9,8},{15,14},{... | collective-permute-start | bytes 1572872 | tf_op jit(solution)/shard_map/ppermute | solution.py:321
  270.2 20.8 %collective-permute-start.38 = (bf16[1,128,2048]{2,1,0:T(8,128)(2,1)}, bf16[1,128,2048]{2,1,0:T(8,128)(2,1)S(1)}, u32[]{:S(2)}, u32[]{:S(2)}) collective-permute-start(bf16[1,128,2048]{2,1,0:T(8,128)(2,1)} %get-tuple-element.72), channel_id=1, source_target_pairs={{0,1},{1,2},{2,3},{4,5},{5,6},{6,7},{8,9},{9,10},{10,11},{12,13},{... | collective-permute-start | bytes 1572872 | tf_op jit(solution)/shard_map/ppermute | solution.py:320
  280.6 19.9 %collective-permute-start.41 = (bf16[1,128,2048]{2,1,0:T(8,128)(2,1)}, bf16[1,128,2048]{2,1,0:T(8,128)(2,1)}, u32[]{:S(2)}, u32[]{:S(2)}) collective-permute-start(bf16[1,128,2048]{2,1,0:T(8,128)(2,1)} %add_convert_fusion.1), channel_id=1, source_target_pairs={{3,2},{2,1},{1,0},{7,6},{6,5},{5,4},{11,10},{10,9},{9,8},{15,14},{... | collective-permute-start | bytes 1572872 | tf_op jit(solution)/shard_map/ppermute | solution.py:321
  (51 other events, 541.1 us)

commit v2 on v1

--- a/solution.py
+++ b/solution.py
@@ -13,6 +13,7 @@
 nothing = -1e30
 pages_per_block = 4
 token_pieces = 2
+projection_parts = (1, 2)
 log2_e = 1.4426950408889634
 
 
@@ -283,45 +284,55 @@
     return lists.astype(jnp.int32), jnp.sum(mine, axis=1).astype(jnp.int32)
 
 
-def place_kernel(source, *refs):
-    terms, out = refs[:-1], refs[-1]
+def place_kernel(position, *refs):
+    terms, kept, sent = refs[:-2], refs[-2], refs[-1]
+    half = len(terms) // 2
     for i, term in enumerate(terms):
-        out[source[i]] = term[...]
-
-
-def place(sources, terms):
+        at = position[i]
+
+        @pl.when(at < half)
+        def _():
+            kept[at] = term[...]
+
+        @pl.when(at >= half)
+        def _():
+            sent[at - half] = term[...]
+
+
+def place(positions, terms):
     tokens, width = terms[0].shape
     vmem = pl.BlockSpec(memory_space=pltpu.VMEM)
+    half = jax.ShapeDtypeStruct((len(terms) // 2, tokens, width), terms[0].dtype)
     return pl.pallas_call(
         place_kernel,
         name="place",
-        out_shape=jax.ShapeDtypeStruct((len(terms), tokens, width), terms[0].dtype),
+        out_shape=(half, half),
         in_specs=[pl.BlockSpec(memory_space=pltpu.SMEM)] + [vmem] * len(terms),
-        out_specs=vmem,
-    )(jnp.stack(sources), *terms)
-
-
-def reduce_line(terms, out_blocks):
+        out_specs=(vmem, vmem),
+    )(jnp.stack(positions), *terms)
+
+
+def halving_position(source, per_chunk, count, index):
+    relative = (source // per_chunk) ^ index
+    reverse, bit = 0, 1
+    while bit < count:
+        reverse = reverse * 2 + relative % 2
+        relative, bit = relative // 2, bit * 2
+    return reverse * per_chunk + source % per_chunk
+
+
+def reduce_halving(kept, sent):
     count = lax.axis_size("tensor")
-    z = lax.axis_index("tensor")
-
-    def chunk(index):
-        index = jnp.clip(index, 0, count - 1)
-        return lax.dynamic_slice_in_dim(terms, index * out_blocks, out_blocks, 0)
-
-    def add(*parts):
-        return functools.reduce(jnp.add, [p.astype(jnp.float32) for p in parts]).astype(terms.dtype)
-
-    up = down = None
-    for step in range(1, count):
-        up_send, down_send = chunk(count - step + z), chunk(z - (count - step))
-        if up is not None:
-            up_send, down_send = add(up_send, up), add(down_send, down)
-        up = lax.ppermute(up_send, "tensor", [(i, i + 1) for i in range(step)])
-        down = lax.ppermute(
-            down_send, "tensor", [(count - 1 - i, count - 2 - i) for i in range(step)]
-        )
-    return add(chunk(z), up, down)
+    distance = 1
+    kept = kept.astype(jnp.float32)
+    while distance < count:
+        arrived = lax.ppermute(sent, "tensor", [(i, i ^ distance) for i in range(count)])
+        distance *= 2
+        kept = kept + arrived.astype(jnp.float32)
+        if distance < count:
+            half = kept.shape[0] // 2
+            kept, sent = kept[:half], kept[half:].astype(sent.dtype)
+    return kept.astype(sent.dtype)
 
 
 def attention_block(queries, suffix_key_value, kv_pages, page_ids, prefix_pages, page_home, out_weight):
@@ -376,20 +387,32 @@
         theirs = swap(theirs, 0, True)
         return combine([mine, theirs, *far[piece]], token)
 
-    def terms_of(piece, s):
-        block = swap(mixed[piece], s, False) if s else mixed[piece]
-        results = []
-        for other in (False, True):
-            here = swap(block, 0, True) if other else block
-            term = jnp.dot(here, out_weight, preferred_element_type=jnp.float32)
-            term = term.astype(jnp.bfloat16)
-            results.append(swap(term, -s, other) if s or other else term)
-        return results
-
-    def reduce_terms(terms):
-        sources = [device_at(s, other) for s in range(chips) for other in (False, True)]
-        placed = place(sources, terms)
-        summed = reduce_line(placed, cache_count // lax.axis_size("tensor"))
+    far_blocks, core_blocks = {}, {}
+
+    def block_of(piece, s, other):
+        if (piece, s) not in far_blocks:
+            here = swap(mixed[piece], s, False) if s else mixed[piece]
+            far_blocks[piece, s] = here
+            core_blocks[piece, s] = swap(here, 0, True)
+        return core_blocks[piece, s] if other else far_blocks[piece, s]
+
+    def term_of(piece, part, s, other):
+        rows = tokens // projection_parts[piece]
+        here = block_of(piece, s, other)[part * rows : (part + 1) * rows]
+        term = jnp.dot(here, out_weight, preferred_element_type=jnp.float32)
+        term = term.astype(jnp.bfloat16)
+        return swap(term, -s, other) if s or other else term
+
+    def reduce_part(piece, part):
+        order = [(s, other) for s in range(chips) for other in (False, True)]
+        terms = [term_of(piece, part, s, other) for s, other in order]
+        count, index = lax.axis_size("tensor"), lax.axis_index("tensor")
+        per_chunk = cache_count // count
+        positions = [
+            halving_position(device_at(s, other), per_chunk, count, index) for s, other in order
+        ]
+        kept, sent = place(positions, terms)
+        summed = reduce_halving(kept, sent)
         return jnp.concatenate([summed[i] for i in range(summed.shape[0])], axis=1)
 
     own, far, mixed = {}, {}, {}
@@ -404,8 +427,9 @@
             token = own[piece][0][1]
         mixed[piece], token = mix(piece, token)
     results = [
-        reduce_terms([term for s in range(chips) for term in terms_of(piece, s)])
+        reduce_part(piece, part)
         for piece in range(token_pieces)
+        for part in range(projection_parts[piece])
     ]
     return jnp.concatenate(results, axis=0)
 

time: 304 us -> 292 us (0.961)
  the two profiles are of different devices: /device:TPU:12 before, /device:TPU:0 now
where the time goes in v2:
time: 292 us; the launch traced here: 290 us
  waiting for transfers between devices  104 us (36%)
  Pallas kernels  86.3 us (30%)
  starting transfers between devices  43.1 us (15%)
  matrix products  32 us (11%)
  other arithmetic  9.11 us (3%)
  local copies, waits for them, and re-layouts  7.94 us (3%)
  blocking collectives  5.99 us (2%)
    pallas_call x4, Pallas kernels, attend(): pl.pallas_call(kernel, name='attend_own' if suffix is not None else 'atte...  66.6 us
    ppermute x6, waiting for transfers between devices, reduce_halving(): lax.ppermute(sent, 'tensor', [(i, i ^ distance) for i in range(count)])  66.3 us
    ppermute x33, waiting for transfers between devices, swap(): return jax.tree.map(lambda leaf: lax.ppermute(leaf, 'cache', pairs), x)  37.7 us
    ppermute x33, starting transfers between devices, swap(): return jax.tree.map(lambda leaf: lax.ppermute(leaf, 'cache', pairs), x)  33.8 us
    dot_general x12, matrix products, term_of(): term = jnp.dot(here, out_weight, preferred_element_type=jnp.float32)  32 us
    pallas_call x4, Pallas kernels, combine(): pl.pallas_call(functools.partial(combine_kernel, parts=len(parts), heads=...  12.1 us
    ppermute x6, starting transfers between devices, reduce_halving(): lax.ppermute(sent, 'tensor', [(i, i ^ distance) for i in range(count)])  9.32 us
    pallas_call x3, Pallas kernels, place(): pl.pallas_call(place_kernel, name='place', out_shape=(half, half), in_spe...  7.67 us
  transfers between devices with their start and end apart: 39, of which 13 were waited for; matrix products, arithmetic and copies ran while one was open for 13% of the time, Pallas kernels for 24%

profile of v2, /device:TPU:0, one launch (start us, length us, event | category | flops | bytes accessed | tf_op | source)
XLA Modules:
  0.0 289.6 jit_solution(10961795771523649142)
XLA Ops:
  1.4 6.0 %all-gather = s32[4,1,65]{2,1,0:T(1,128)S(1)} all-gather(s32[1,1,65]{2,1,0:T(1,128)S(1)} %add_bitcast_fusion), channel_id=1, replica_groups=mesh['groups'=2,'cache'=4,'tensor'=4] {'cache'}, dimensions={0}, use_global_device_ids=true | all-gather | bytes 1300 | tf_op jit(solution)/shard_map/all_gather | solution.py:273
  15.3 17.0 %attend_own.2 = (bf16[128,2048]{1,0:T(8,128)(2,1)}, bf16[128,2048]{1,0:T(8,128)(2,1)}, f32[16,128]{1,0:T(8,128)}, f32[16,128]{1,0:T(8,128)}) custom-call(s32[2]{0:T(128)} %pad_add_fusion.1.which, s32[4,64]{1,0:T(4,128)} %select_reduce_fusion.1.lists, s32[4]{0:T(128)} %get-tuple-element.77.counts.token, s32[4]{0:T(128)} %get-tuple-element.77.counts.token, ...), custom_call_target="tpu_custom_call" | custom-call | flops 10000000000 | bytes 6000000 | tf_op jit(solution)/shard_map/attend_own/pallas_call | solution.py:207
  35.0 16.2 %attend.2 = (bf16[128,2048]{1,0:T(8,128)(2,1)}, bf16[128,2048]{1,0:T(8,128)(2,1)}, f32[16,128]{1,0:T(8,128)}, f32[16,128]{1,0:T(8,128)}) custom-call(s32[2]{0:T(128)} %pad_add_fusion.2.which, s32[4,64]{1,0:T(4,128)} %select_reduce_fusion.1.lists, s32[4]{0:T(128)} %get-tuple-element.77.counts.token, f32[16,128]{1,0:T(8,128)} %get-tuple-element.47.token.refs_3_, ...), custom_call_target="tpu_custom_call" | custom-call | flops 10000000000 | bytes 6000000 | tf_op jit(solution)/shard_map/attend/pallas_call | solution.py:207
  55.0 2.8 combine.4
  58.5 16.3 %attend.3 = (bf16[128,2048]{1,0:T(8,128)(2,1)}, bf16[128,2048]{1,0:T(8,128)(2,1)}, f32[16,128]{1,0:T(8,128)}, f32[16,128]{1,0:T(8,128)}) custom-call(s32[2]{0:T(128)} %pad_add_fusion.2.which, s32[4,64]{1,0:T(4,128)} %select_reduce_fusion.1.lists, s32[4]{0:T(128)} %get-tuple-element.77.counts.token, f32[16,128]{1,0:T(8,128)} %get-tuple-element.53.token, ...), custom_call_target="tpu_custom_call" | custom-call | flops 10000000000 | bytes 6000000 | tf_op jit(solution)/shard_map/attend/pallas_call | solution.py:207
  75.4 17.7 %collective-permute-start.10 = (bf16[128,2048]{1,0:T(8,128)(2,1)S(1)}, bf16[128,2048]{1,0:T(8,128)(2,1)S(1)}, u32[]{:S(2)}, u32[]{:S(2)}) collective-permute-start(bf16[128,2048]{1,0:T(8,128)(2,1)S(1)} %copy-done.11), channel_id=1, source_target_pairs={{0,8},{4,12},{8,0},{12,4},{1,9},{5,13},{9,1},{13,5},{2,10},{6,14},... | collective-permute-start | bytes 1572872 | tf_op jit(solution)/shard_map/ppermute | solution.py:352
  96.4 2.7 combine.5
  100.0 5.5 %collective-permute-done.12.refs_5_ = f32[16,128]{1,0:T(8,128)S(1)} collective-permute-done((f32[16,128]{1,0:T(8,128)S(1)}, f32[16,128]{1,0:T(8,128)S(1)}, u32[]{:S(2)}, u32[]{:S(2)}) %collective-permute-start.12) | collective-permute-done | bytes 8224 | tf_op jit(solution)/shard_map/ppermute | solution.py:352
  106.9 3.3 %combine.6 = (bf16[128,2048]{1,0:T(8,128)(2,1)}, f32[16,128]{1,0:T(8,128)}) custom-call(f32[16,128]{1,0:T(8,128)} %get-tuple-element.58.token, bf16[128,2048]{1,0:T(8,128)(2,1)} %get-tuple-element.59.refs_0_, bf16[128,2048]{1,0:T(8,128)(2,1)} %copy-done.13, bf16[128,2048]{1,0:T(8,128)(2,1)} %copy-done.14, f32[16,128]{1,0:T(8,128)} %get-tuple-element.47.token.refs_3_, ...), custom_call_target="tpu_custom_call" | custom-call | flops 1000000000 | bytes 3000000 | tf_op jit(solution)/shard_map/combine/pallas_call | solution.py:254
  111.0 17.1 %attend_own.3 = (bf16[128,2048]{1,0:T(8,128)(2,1)}, bf16[128,2048]{1,0:T(8,128)(2,1)}, f32[16,128]{1,0:T(8,128)}, f32[16,128]{1,0:T(8,128)}) custom-call(s32[2]{0:T(128)} %pad_add_fusion.1.which, s32[4,64]{1,0:T(4,128)} %select_reduce_fusion.1.lists, s32[4]{0:T(128)} %get-tuple-element.77.counts.token, f32[16,128]{1,0:T(8,128)} %get-tuple-element.66.token, ...), custom_call_target="tpu_custom_call" | custom-call | flops 10000000000 | bytes 6000000 | tf_op jit(solution)/shard_map/attend_own/pallas_call | solution.py:207
  128.9 5.4 %convolution_convert_fusion.3.refs_0_ = bf16[128,2048]{1,0:T(8,128)(2,1)} fusion(bf16[128,2048]{1,0:T(8,128)(2,1)S(1)} %copy-done.1, bf16[2048,2048]{1,0:T(8,128)(2,1)} %param.13), kind=kOutput, calls=%fused_computation.3 | convolution fusion | flops 1074003968 | bytes 9437184 | tf_op jit(solution)/shard_map/dot_general | solution.py:402
  136.3 6.8 %collective-permute-done.23.refs_2_ = bf16[128,2048]{1,0:T(8,128)(2,1)S(1)} collective-permute-done((bf16[128,2048]{1,0:T(8,128)(2,1)S(1)}, bf16[128,2048]{1,0:T(8,128)(2,1)S(1)}, u32[]{:S(2)}, u32[]{:S(2)}) %collective-permute-start.23) | collective-permute-done | bytes 524320 | tf_op jit(solution)/shard_map/ppermute | solution.py:352
  143.9 3.3 %combine.7 = (bf16[128,2048]{1,0:T(8,128)(2,1)}, f32[16,128]{1,0:T(8,128)}) custom-call(f32[16,128]{1,0:T(8,128)} %get-tuple-element.67.token.refs_3_, bf16[128,2048]{1,0:T(8,128)(2,1)} %get-tuple-element.68.refs_0_, bf16[128,2048]{1,0:T(8,128)(2,1)} %copy-done.20, bf16[128,2048]{1,0:T(8,128)(2,1)} %copy-done.21, f32[16,128]{1,0:T(8,128)} %get-tuple-element.67.token.refs_3_, ...), custom_call_target="tpu_custom_call" | custom-call | flops 1000000000 | bytes 3000000 | tf_op jit(solution)/shard_map/combine/pallas_call | solution.py:254
  147.4 4.8 %convolution_convert_fusion.2 = bf16[128,2048]{1,0:T(8,128)(2,1)S(1)} fusion(bf16[128,2048]{1,0:T(8,128)(2,1)S(1)} %collective-permute-done.13, bf16[2048,2048]{1,0:T(8,128)(2,1)} %param.13), kind=kOutput, calls=%fused_computation.2 | convolution fusion | flops 1074003968 | bytes 9437184 | tf_op jit(solution)/shard_map/dot_general | solution.py:402
  160.3 5.3 %collective-permute-done.28 = bf16[128,2048]{1,0:T(8,128)(2,1)S(1)} collective-permute-done((bf16[128,2048]{1,0:T(8,128)(2,1)}, bf16[128,2048]{1,0:T(8,128)(2,1)S(1)}, u32[]{:S(2)}, u32[]{:S(2)}) %collective-permute-start.28) | collective-permute-done | bytes 524320 | tf_op jit(solution)/shard_map/ppermute | solution.py:352
  170.2 2.5 convolution_convert_fusion.9
  179.0 13.6 %collective-permute-done.18.refs_3_ = bf16[128,2048]{1,0:T(8,128)(2,1)S(1)} collective-permute-done((bf16[128,2048]{1,0:T(8,128)(2,1)S(1)}, bf16[128,2048]{1,0:T(8,128)(2,1)S(1)}, u32[]{:S(2)}, u32[]{:S(2)}) %collective-permute-start.18) | collective-permute-done | bytes 524320 | tf_op jit(solution)/shard_map/ppermute | solution.py:352
  193.4 3.1 %place.3 = (bf16[2,128,2048]{2,1,0:T(8,128)(2,1)}, bf16[2,128,2048]{2,1,0:T(8,128)(2,1)}) custom-call(s32[4]{0:T(128)} %pad_add_fusion.position, bf16[128,2048]{1,0:T(8,128)(2,1)} %convolution_convert_fusion.3.refs_0_, bf16[128,2048]{1,0:T(8,128)(2,1)} %copy-done.3, bf16[128,2048]{1,0:T(8,128)(2,1)} %copy-done.4, bf16[128,2048]{1,0:T(8,128)(2,1)} %copy-done.5), custom_call_target="tpu_custom_call" | custom-call | tf_op jit(solution)/shard_map/place/pallas_call | solution.py:306
  202.7 5.7 %convolution_convert_fusion.11.refs_0_ = bf16[64,2048]{1,0:T(8,128)(2,1)} fusion(bf16[2048,2048]{1,0:T(8,128)(2,1)} %param.13, bf16[128,2048]{1,0:T(8,128)(2,1)S(1)} %copy-done), kind=kOutput, calls=%fused_computation.11 | convolution fusion | flops 537001984 | bytes 8912896 | tf_op jit(solution)/shard_map/dot_general | solution.py:402
  213.4 22.5 %collective-permute-done.37 = bf16[2,64,2048]{2,1,0:T(8,128)(2,1)} collective-permute-done((bf16[2,64,2048]{2,1,0:T(8,128)(2,1)}, bf16[2,64,2048]{2,1,0:T(8,128)(2,1)}, u32[]{:S(2)}, u32[]{:S(2)}) %collective-permute-start.37) | collective-permute-done | bytes 524320 | tf_op jit(solution)/shard_map/ppermute | solution.py:329
  237.2 2.7 collective-permute-start.38
  239.8 11.4 %collective-permute-done.32 = bf16[2,64,2048]{2,1,0:T(8,128)(2,1)S(1)} collective-permute-done((bf16[2,64,2048]{2,1,0:T(8,128)(2,1)}, bf16[2,64,2048]{2,1,0:T(8,128)(2,1)S(1)}, u32[]{:S(2)}, u32[]{:S(2)}) %collective-permute-start.32) | collective-permute-done | bytes 524320 | tf_op jit(solution)/shard_map/ppermute | solution.py:329
  256.0 22.2 %collective-permute-done.33 = bf16[1,64,2048]{2,1,0:T(8,128)(2,1)S(1)} collective-permute-done((bf16[1,64,2048]{2,1,0:T(8,128)(2,1)S(1)}, bf16[1,64,2048]{2,1,0:T(8,128)(2,1)S(1)}, u32[]{:S(2)}, u32[]{:S(2)}) %collective-permute-start.33) | collective-permute-done | bytes 262176 | tf_op jit(solution)/shard_map/ppermute | solution.py:329
  278.3 10.1 %collective-permute-done.20 = bf16[1,128,2048]{2,1,0:T(8,128)(2,1)S(1)} collective-permute-done((bf16[1,128,2048]{2,1,0:T(8,128)(2,1)S(1)}, bf16[1,128,2048]{2,1,0:T(8,128)(2,1)S(1)}, u32[]{:S(2)}, u32[]{:S(2)}) %collective-permute-start.20) | collective-permute-done | bytes 524320 | tf_op jit(solution)/shard_map/ppermute | solution.py:329
  (168 shorter events, 64.5 us)
Async XLA Ops:
  11.8 20.5 %collective-permute-start = (bf16[128,2048]{1,0:T(8,128)(2,1)S(1)}, bf16[128,2048]{1,0:T(8,128)(2,1)S(1)}, u32[]{:S(2)}, u32[]{:S(2)}) collective-permute-start(bf16[128,2048]{1,0:T(8,128)(2,1)S(1)} %get-tuple-element.81.refs_0_), channel_id=1, source_target_pairs={{0,8},{4,12},{8,0},{12,4},{1,9},{5,13},{9,1},{13,5},{2,10},{6,14},... | collective-permute-start | bytes 1572872 | tf_op jit(solution)/shard_map/ppermute | solution.py:352
  32.4 18.9 %collective-permute-start.5 = (bf16[128,2048]{1,0:T(8,128)(2,1)S(1)}, bf16[128,2048]{1,0:T(8,128)(2,1)S(1)}, u32[]{:S(2)}, u32[]{:S(2)}) collective-permute-start(bf16[128,2048]{1,0:T(8,128)(2,1)S(1)} %get-tuple-element.80.refs_0_), channel_id=1, source_target_pairs={{0,8},{4,12},{8,0},{12,4},{1,9},{5,13},{9,1},{13,5},{2,10},{6,14},... | collective-permute-start | bytes 1572872 | tf_op jit(solution)/shard_map/ppermute | solution.py:352
  74.8 20.4 %collective-permute-start.7 = (bf16[128,2048]{1,0:T(8,128)(2,1)}, bf16[128,2048]{1,0:T(8,128)(2,1)}, u32[]{:S(2)}, u32[]{:S(2)}) collective-permute-start(bf16[128,2048]{1,0:T(8,128)(2,1)} %get-tuple-element.55), channel_id=1, source_target_pairs={{0,4},{4,0},{8,12},{12,8},{1,5},{5,1},{9,13},{13,9},{2,6},{6,2},{1... | collective-permute-start | bytes 1572872 | tf_op jit(solution)/shard_map/ppermute | solution.py:352
  74.9 25.1 %collective-permute-start.9 = (bf16[128,2048]{1,0:T(8,128)(2,1)S(1)}, bf16[128,2048]{1,0:T(8,128)(2,1)S(1)}, u32[]{:S(2)}, u32[]{:S(2)}) collective-permute-start(bf16[128,2048]{1,0:T(8,128)(2,1)S(1)} %copy-done.10), channel_id=1, source_target_pairs={{0,4},{4,0},{8,12},{12,8},{1,5},{5,1},{9,13},{13,9},{2,6},{6,2},{1... | collective-permute-start | bytes 1572872 | tf_op jit(solution)/shard_map/ppermute | solution.py:352
  75.4 30.1 %collective-permute-start.10 = (bf16[128,2048]{1,0:T(8,128)(2,1)S(1)}, bf16[128,2048]{1,0:T(8,128)(2,1)S(1)}, u32[]{:S(2)}, u32[]{:S(2)}) collective-permute-start(bf16[128,2048]{1,0:T(8,128)(2,1)S(1)} %copy-done.11), channel_id=1, source_target_pairs={{0,8},{4,12},{8,0},{12,4},{1,9},{5,13},{9,1},{13,5},{2,10},{6,14},... | collective-permute-start | bytes 1572872 | tf_op jit(solution)/shard_map/ppermute | solution.py:352
  93.1 17.1 %collective-permute-start.21 = (bf16[128,2048]{1,0:T(8,128)(2,1)S(1)}, bf16[128,2048]{1,0:T(8,128)(2,1)S(1)}, u32[]{:S(2)}, u32[]{:S(2)}) collective-permute-start(bf16[128,2048]{1,0:T(8,128)(2,1)S(1)} %get-tuple-element.80.refs_0_), channel_id=1, source_target_pairs={{0,4},{4,0},{8,12},{12,8},{1,5},{5,1},{9,13},{13,9},{2,6},{6,2},{1... | collective-permute-start | bytes 1572872 | tf_op jit(solution)/shard_map/ppermute | solution.py:352
  99.1 37.2 %collective-permute-start.25 = (f32[16,128]{1,0:T(8,128)}, f32[16,128]{1,0:T(8,128)S(1)}, u32[]{:S(2)}, u32[]{:S(2)}) collective-permute-start(f32[16,128]{1,0:T(8,128)} %get-tuple-element.58.token), channel_id=1, source_target_pairs={{0,8},{4,12},{8,0},{12,4},{1,9},{5,13},{9,1},{13,5},{2,10},{6,14},... | collective-permute-start | bytes 24584 | tf_op jit(solution)/shard_map/ppermute | solution.py:352
  128.8 18.6 %collective-permute-start.13 = (bf16[128,2048]{1,0:T(8,128)(2,1)S(1)}, bf16[128,2048]{1,0:T(8,128)(2,1)S(1)}, u32[]{:S(2)}, u32[]{:S(2)}) collective-permute-start(bf16[128,2048]{1,0:T(8,128)(2,1)S(1)} %copy-done.1), channel_id=1, source_target_pairs={{0,4},{4,0},{8,12},{12,8},{1,5},{5,1},{9,13},{13,9},{2,6},{6,2},{1... | collective-permute-start | bytes 1572872 | tf_op jit(solution)/shard_map/ppermute | solution.py:352
  134.4 20.0 %collective-permute-start.15 = (bf16[128,2048]{1,0:T(8,128)(2,1)S(1)}, bf16[128,2048]{1,0:T(8,128)(2,1)S(1)}, u32[]{:S(2)}, u32[]{:S(2)}) collective-permute-start(bf16[128,2048]{1,0:T(8,128)(2,1)S(1)} %copy-done.1), channel_id=1, source_target_pairs={{0,8},{4,12},{8,0},{12,4},{1,9},{5,13},{9,1},{13,5},{2,10},{6,14},... | collective-permute-start | bytes 1572872 | tf_op jit(solution)/shard_map/ppermute | solution.py:352
  147.3 18.3 %collective-permute-start.28 = (bf16[128,2048]{1,0:T(8,128)(2,1)}, bf16[128,2048]{1,0:T(8,128)(2,1)S(1)}, u32[]{:S(2)}, u32[]{:S(2)}) collective-permute-start(bf16[128,2048]{1,0:T(8,128)(2,1)} %get-tuple-element.72), channel_id=1, source_target_pairs={{0,8},{4,12},{8,0},{12,4},{1,9},{5,13},{9,1},{13,5},{2,10},{6,14},... | collective-permute-start | bytes 1572872 | tf_op jit(solution)/shard_map/ppermute | solution.py:352
  152.2 24.2 %collective-permute-start.14 = (bf16[128,2048]{1,0:T(8,128)(2,1)S(1)}, bf16[128,2048]{1,0:T(8,128)(2,1)S(1)}, u32[]{:S(2)}, u32[]{:S(2)}) collective-permute-start(bf16[128,2048]{1,0:T(8,128)(2,1)S(1)} %convolution_convert_fusion.2), channel_id=1, source_target_pairs={{0,4},{4,0},{8,12},{12,8},{1,5},{5,1},{9,13},{13,9},{2,6},{6,2},{1... | collective-permute-start | bytes 1572872 | tf_op jit(solution)/shard_map/ppermute | solution.py:352
  155.7 23.1 %collective-permute-start.16 = (bf16[128,2048]{1,0:T(8,128)(2,1)S(1)}, bf16[128,2048]{1,0:T(8,128)(2,1)S(1)}, u32[]{:S(2)}, u32[]{:S(2)}) collective-permute-start(bf16[128,2048]{1,0:T(8,128)(2,1)S(1)} %convolution_convert_fusion.1), channel_id=1, source_target_pairs={{0,8},{4,12},{8,0},{12,4},{1,9},{5,13},{9,1},{13,5},{2,10},{6,14},... | collective-permute-start | bytes 1572872 | tf_op jit(solution)/shard_map/ppermute | solution.py:352
  159.9 36.5 %collective-permute-start.34 = (bf16[64,2048]{1,0:T(8,128)(2,1)S(1)}, bf16[64,2048]{1,0:T(8,128)(2,1)S(1)}, u32[]{:S(2)}, u32[]{:S(2)}) collective-permute-start(bf16[64,2048]{1,0:T(8,128)(2,1)S(1)} %convolution_convert_fusion.6), channel_id=1, source_target_pairs={{0,4},{4,0},{8,12},{12,8},{1,5},{5,1},{9,13},{13,9},{2,6},{6,2},{1... | collective-permute-start | bytes 786440 | tf_op jit(solution)/shard_map/ppermute | solution.py:352
  167.2 31.2 %collective-permute-start.35 = (bf16[64,2048]{1,0:T(8,128)(2,1)S(1)}, bf16[64,2048]{1,0:T(8,128)(2,1)}, u32[]{:S(2)}, u32[]{:S(2)}) collective-permute-start(bf16[64,2048]{1,0:T(8,128)(2,1)S(1)} %convolution_convert_fusion.5), channel_id=1, source_target_pairs={{0,8},{4,12},{8,0},{12,4},{1,9},{5,13},{9,1},{13,5},{2,10},{6,14},... | collective-permute-start | bytes 786440 | tf_op jit(solution)/shard_map/ppermute | solution.py:352
  172.7 19.8 %collective-permute-start.18 = (bf16[128,2048]{1,0:T(8,128)(2,1)S(1)}, bf16[128,2048]{1,0:T(8,128)(2,1)S(1)}, u32[]{:S(2)}, u32[]{:S(2)}) collective-permute-start(bf16[128,2048]{1,0:T(8,128)(2,1)S(1)} %convolution_convert_fusion), channel_id=1, source_target_pairs={{0,12},{4,8},{8,4},{12,0},{1,13},{5,9},{9,5},{13,1},{2,14},{6,10},... | collective-permute-start | bytes 1572872 | tf_op jit(solution)/shard_map/ppermute | solution.py:352
  176.5 23.5 %collective-permute-start.36 = (bf16[64,2048]{1,0:T(8,128)(2,1)S(1)}, bf16[64,2048]{1,0:T(8,128)(2,1)}, u32[]{:S(2)}, u32[]{:S(2)}) collective-permute-start(bf16[64,2048]{1,0:T(8,128)(2,1)S(1)} %convolution_convert_fusion.4), channel_id=1, source_target_pairs={{0,12},{4,8},{8,4},{12,0},{1,13},{5,9},{9,5},{13,1},{2,14},{6,10},... | collective-permute-start | bytes 786440 | tf_op jit(solution)/shard_map/ppermute | solution.py:352
  178.8 29.6 %collective-permute-start.27 = (bf16[64,2048]{1,0:T(8,128)(2,1)S(1)}, bf16[64,2048]{1,0:T(8,128)(2,1)}, u32[]{:S(2)}, u32[]{:S(2)}) collective-permute-start(bf16[64,2048]{1,0:T(8,128)(2,1)S(1)} %convolution_convert_fusion.10), channel_id=1, source_target_pairs={{0,4},{4,0},{8,12},{12,8},{1,5},{5,1},{9,13},{13,9},{2,6},{6,2},{1... | collective-permute-start | bytes 786440 | tf_op jit(solution)/shard_map/ppermute | solution.py:352
  192.6 15.8 %collective-permute-start.29 = (bf16[64,2048]{1,0:T(8,128)(2,1)}, bf16[64,2048]{1,0:T(8,128)(2,1)}, u32[]{:S(2)}, u32[]{:S(2)}) collective-permute-start(bf16[64,2048]{1,0:T(8,128)(2,1)} %convolution_convert_fusion.9), channel_id=1, source_target_pairs={{0,8},{4,12},{8,0},{12,4},{1,9},{5,13},{9,1},{13,5},{2,10},{6,14},... | collective-permute-start | bytes 786440 | tf_op jit(solution)/shard_map/ppermute | solution.py:352
  198.4 56.0 %collective-permute-start.19 = (bf16[2,128,2048]{2,1,0:T(8,128)(2,1)}, bf16[2,128,2048]{2,1,0:T(8,128)(2,1)S(1)}, u32[]{:S(2)}, u32[]{:S(2)}) collective-permute-start(bf16[2,128,2048]{2,1,0:T(8,128)(2,1)} %get-tuple-element.65), channel_id=1, source_target_pairs={{0,1},{1,0},{2,3},{3,2},{4,5},{5,4},{6,7},{7,6},{8,9},{9,8},{10,11... | collective-permute-start | bytes 3145736 | tf_op jit(solution)/shard_map/ppermute | solution.py:329
  202.3 33.7 %collective-permute-start.37 = (bf16[2,64,2048]{2,1,0:T(8,128)(2,1)}, bf16[2,64,2048]{2,1,0:T(8,128)(2,1)}, u32[]{:S(2)}, u32[]{:S(2)}) collective-permute-start(bf16[2,64,2048]{2,1,0:T(8,128)(2,1)} %get-tuple-element.76), channel_id=1, source_target_pairs={{0,1},{1,0},{2,3},{3,2},{4,5},{5,4},{6,7},{7,6},{8,9},{9,8},{10,11... | collective-permute-start | bytes 1572872 | tf_op jit(solution)/shard_map/ppermute | solution.py:329
  211.9 39.4 %collective-permute-start.32 = (bf16[2,64,2048]{2,1,0:T(8,128)(2,1)}, bf16[2,64,2048]{2,1,0:T(8,128)(2,1)S(1)}, u32[]{:S(2)}, u32[]{:S(2)}) collective-permute-start(bf16[2,64,2048]{2,1,0:T(8,128)(2,1)} %get-tuple-element.74), channel_id=1, source_target_pairs={{0,1},{1,0},{2,3},{3,2},{4,5},{5,4},{6,7},{7,6},{8,9},{9,8},{10,11... | collective-permute-start | bytes 1572872 | tf_op jit(solution)/shard_map/ppermute | solution.py:329
  237.2 18.8 %collective-permute-start.38 = (bf16[1,64,2048]{2,1,0:T(8,128)(2,1)S(1)}, bf16[1,64,2048]{2,1,0:T(8,128)(2,1)S(1)}, u32[]{:S(2)}, u32[]{:S(2)}) collective-permute-start(bf16[1,64,2048]{2,1,0:T(8,128)(2,1)S(1)} %slice.126), channel_id=1, source_target_pairs={{0,2},{1,3},{2,0},{3,1},{4,6},{5,7},{6,4},{7,5},{8,10},{9,11},{10,... | collective-permute-start | bytes 786440 | tf_op jit(solution)/shard_map/ppermute | solution.py:329
  252.5 25.7 %collective-permute-start.33 = (bf16[1,64,2048]{2,1,0:T(8,128)(2,1)S(1)}, bf16[1,64,2048]{2,1,0:T(8,128)(2,1)S(1)}, u32[]{:S(2)}, u32[]{:S(2)}) collective-permute-start(bf16[1,64,2048]{2,1,0:T(8,128)(2,1)S(1)} %slice.127), channel_id=1, source_target_pairs={{0,2},{1,3},{2,0},{3,1},{4,6},{5,7},{6,4},{7,5},{8,10},{9,11},{10,... | collective-permute-start | bytes 786440 | tf_op jit(solution)/shard_map/ppermute | solution.py:329
  254.8 33.6 %collective-permute-start.20 = (bf16[1,128,2048]{2,1,0:T(8,128)(2,1)S(1)}, bf16[1,128,2048]{2,1,0:T(8,128)(2,1)S(1)}, u32[]{:S(2)}, u32[]{:S(2)}) collective-permute-start(bf16[1,128,2048]{2,1,0:T(8,128)(2,1)S(1)} %slice.125), channel_id=1, source_target_pairs={{0,2},{1,3},{2,0},{3,1},{4,6},{5,7},{6,4},{7,5},{8,10},{9,11},{10,... | collective-permute-start | bytes 1572872 | tf_op jit(solution)/shard_map/ppermute | solution.py:329
  (49 other events, 519.9 us)
